TPU v7x, 16 devices: a 4x2x1 block of a 4x4x8 slice. The times are simulated.
16 devices in a mesh: dp: 2 (over y, z), sp: 8 (over x, core).
Axes of the slice: x: 4, y: 2, z: 1, core: 2. Of those that a mesh axis runs over, the one named last changes fastest.
The devices are a block of a 4x4x8 slice.
Arguments:
- hidden: bfloat16 [12288, 2048], P(('dp', 'sp')), parts along dimension 0
- positions: int32 [12288], P(('dp', 'sp')), parts along dimension 0
- d_attn: bfloat16 [12288, 2048], P(('dp', 'sp')), parts along dimension 0
- ln_weight: bfloat16 [2048], replicated
- w_q: bfloat16 [2048, 2048], replicated
- w_k: bfloat16 [2048, 2048], replicated
- w_v: bfloat16 [2048, 2048], replicated
- w_o: bfloat16 [2048, 2048], replicated
Outputs:
- output 1: bfloat16 [12288, 2048], P(('dp', 'sp')), parts along dimension 0
- output 2: bfloat16 [12288, 2048], P(('dp', 'sp')), parts along dimension 0
- output 3: bfloat16 [4096], P('dp'), parts along dimension 0
- output 4: bfloat16 [4096, 2048], P('dp'), parts along dimension 0
- output 5: bfloat16 [4096, 2048], P('dp'), parts along dimension 0
- output 6: bfloat16 [4096, 2048], P('dp'), parts along dimension 0
- output 7: bfloat16 [4096, 2048], P('dp'), parts along dimension 0
There are 2 independent parts. A program takes and returns all parts, laid end to end along the dimension named above; an argument that names none is the same for every part.
All inputs are finite; a program needn't handle non-finite values.
Results may differ from a plain program's by a relative error of at most 0.0122721.
Values are sent between devices in bfloat16 or wider.
A program may use at most 768 MiB of HBM per device.

v0:
```python
import math
import jax
import jax.numpy as jnp
from jax import lax
from jax.sharding import PartitionSpec as P

HEAD_DIM = 128
LN_EPS = 1e-5
ROPE_BASE = 10000.0


def norm_f32(hid_f32, weight_f32):
    mean_val = jnp.mean(hid_f32, axis=-1, keepdims=True)
    centered = hid_f32 - mean_val
    var_val = jnp.mean(centered * centered, axis=-1, keepdims=True)
    return centered * lax.rsqrt(var_val + LN_EPS) * weight_f32


def rope_tables(positions):
    inv_freq = ROPE_BASE ** (-jnp.arange(0, HEAD_DIM, 2, dtype=jnp.float32) / HEAD_DIM)
    angles = positions.astype(jnp.float32)[:, None] * inv_freq[None, :]
    return jnp.cos(angles)[:, None, :], jnp.sin(angles)[:, None, :]


def apply_rope(values, cos_t, sin_t):
    rot_pairs = values.reshape(values.shape[:-1] + (HEAD_DIM // 2, 2))
    even_part = rot_pairs[..., 0]
    odd_part = rot_pairs[..., 1]
    new_even = even_part * cos_t - odd_part * sin_t
    new_odd = odd_part * cos_t + even_part * sin_t
    return jnp.stack([new_even, new_odd], axis=-1).reshape(values.shape)


def block_probs(q_block, row_start, k_all):
    scores = jnp.einsum('qgrd,kgd->grqk', q_block, k_all, preferred_element_type=jnp.float32) * (HEAD_DIM ** -0.5)
    row_ids = row_start + jnp.arange(q_block.shape[0])
    col_ids = jnp.arange(k_all.shape[0])
    scores = jnp.where(row_ids[:, None] >= col_ids[None, :], scores, -jnp.inf)
    return jax.nn.softmax(scores, axis=-1)


def attn_forward(q_grp, k_all, v_all, row_offset):
    n_rows = q_grp.shape[0]
    block_rows = math.gcd(n_rows, 128)
    q_blocks = q_grp.reshape((n_rows // block_rows, block_rows) + q_grp.shape[1:])

    def one_block(block_in):
        q_block, block_idx = block_in
        attn_prob = block_probs(q_block, row_offset + block_idx * block_rows, k_all)
        return jnp.einsum('grqk,kgd->qgrd', attn_prob.astype(jnp.bfloat16), v_all, preferred_element_type=jnp.float32).astype(jnp.bfloat16)

    o_blocks = lax.map(one_block, (q_blocks, jnp.arange(n_rows // block_rows)))
    return o_blocks.reshape(q_grp.shape)


def attn_backward(q_grp, k_all, v_all, do_grp, row_offset):
    n_rows = q_grp.shape[0]
    block_rows = math.gcd(n_rows, 128)
    block_shape = (n_rows // block_rows, block_rows) + q_grp.shape[1:]

    def one_block(carry, block_in):
        dk_acc, dv_acc = carry
        q_block, do_block, block_idx = block_in
        attn_prob = block_probs(q_block, row_offset + block_idx * block_rows, k_all)
        d_prob = jnp.einsum('qgrd,kgd->grqk', do_block, v_all, preferred_element_type=jnp.float32)
        row_dot = jnp.sum(attn_prob * d_prob, axis=-1, keepdims=True)
        d_score = (attn_prob * (d_prob - row_dot) * (HEAD_DIM ** -0.5)).astype(jnp.bfloat16)
        dq_block = jnp.einsum('grqk,kgd->qgrd', d_score, k_all, preferred_element_type=jnp.float32).astype(jnp.bfloat16)
        dk_acc = dk_acc + jnp.einsum('grqk,qgrd->kgd', d_score, q_block, preferred_element_type=jnp.float32)
        dv_acc = dv_acc + jnp.einsum('grqk,qgrd->kgd', attn_prob.astype(jnp.bfloat16), do_block, preferred_element_type=jnp.float32)
        return (dk_acc, dv_acc), dq_block

    zero_acc = jnp.zeros(k_all.shape, jnp.float32)
    kv_sums, dq_blocks = lax.scan(one_block, (zero_acc, zero_acc), (q_grp.reshape(block_shape), do_grp.reshape(block_shape), jnp.arange(block_shape[0])))
    return dq_blocks.reshape(q_grp.shape), kv_sums[0], kv_sums[1]


def solution(mesh):
    sp_size = mesh.shape['sp']
    row_spec = P(('dp', 'sp'), None)
    pos_spec = P(('dp', 'sp'))
    full_spec = P(None, None)
    grad_spec = P('dp', None)

    def local_step(hidden, positions, d_attn, ln_weight, w_q, w_k, w_v, w_o):
        local_rows = hidden.shape[0]
        n_heads = w_q.shape[1] // HEAD_DIM
        kv_heads = w_k.shape[1] // HEAD_DIM
        copies = max(sp_size // kv_heads, 1)
        normed32, norm_vjp = jax.vjp(norm_f32, hidden.astype(jnp.float32), ln_weight.astype(jnp.float32))
        normed = normed32.astype(jnp.bfloat16)
        cos_t, sin_t = rope_tables(positions)
        q_rot = apply_rope(jnp.dot(normed, w_q, preferred_element_type=jnp.float32).reshape(local_rows, n_heads, HEAD_DIM), cos_t, sin_t).astype(jnp.bfloat16)
        k_rot = apply_rope(jnp.dot(normed, w_k, preferred_element_type=jnp.float32).reshape(local_rows, kv_heads, HEAD_DIM), cos_t, sin_t).astype(jnp.bfloat16)
        v_loc = jnp.dot(normed, w_v, preferred_element_type=jnp.float32).astype(jnp.bfloat16).reshape(local_rows, kv_heads, HEAD_DIM)
        if copies > 1:
            k_rot = jnp.repeat(k_rot, copies, axis=1)
            v_loc = jnp.repeat(v_loc, copies, axis=1)
        q_heads = lax.all_to_all(q_rot, 'sp', 1, 0, tiled=True)
        k_heads = lax.all_to_all(k_rot, 'sp', 1, 0, tiled=True)
        v_heads = lax.all_to_all(v_loc, 'sp', 1, 0, tiled=True)
        seq_rows, heads_local = q_heads.shape[0], q_heads.shape[1]
        kv_local = k_heads.shape[1]
        q_grp = q_heads.reshape(seq_rows, kv_local, heads_local // kv_local, HEAD_DIM)
        o_grp = attn_forward(q_grp, k_heads, v_heads, 0)
        o_tok = lax.all_to_all(o_grp.reshape(q_heads.shape), 'sp', 0, 1, tiled=True).reshape(local_rows, n_heads * HEAD_DIM)
        attn_out = jnp.dot(o_tok, w_o, preferred_element_type=jnp.float32).astype(jnp.bfloat16)
        d_o = jnp.einsum('td,ed->te', d_attn, w_o, preferred_element_type=jnp.float32).astype(jnp.bfloat16)
        dw_o = jnp.einsum('te,td->ed', o_tok, d_attn, preferred_element_type=jnp.float32)
        do_heads = lax.all_to_all(d_o.reshape(local_rows, n_heads, HEAD_DIM), 'sp', 1, 0, tiled=True)
        dq_grp, dk_acc, dv_acc = attn_backward(q_grp, k_heads, v_heads, do_heads.reshape(q_grp.shape), 0)
        dq_tok = lax.all_to_all(dq_grp.reshape(q_heads.shape), 'sp', 0, 1, tiled=True)
        dk_tok = lax.all_to_all(dk_acc.astype(jnp.bfloat16), 'sp', 0, 1, tiled=True)
        dv_tok = lax.all_to_all(dv_acc.astype(jnp.bfloat16), 'sp', 0, 1, tiled=True)
        if copies > 1:
            dk_tok = dk_tok.reshape(local_rows, kv_heads, copies, HEAD_DIM).astype(jnp.float32).sum(axis=2).astype(jnp.bfloat16)
            dv_tok = dv_tok.reshape(local_rows, kv_heads, copies, HEAD_DIM).astype(jnp.float32).sum(axis=2).astype(jnp.bfloat16)
        g_q = apply_rope(dq_tok.astype(jnp.float32), cos_t, -sin_t).astype(jnp.bfloat16).reshape(local_rows, n_heads * HEAD_DIM)
        g_k = apply_rope(dk_tok.astype(jnp.float32), cos_t, -sin_t).astype(jnp.bfloat16).reshape(local_rows, kv_heads * HEAD_DIM)
        g_v = dv_tok.reshape(local_rows, kv_heads * HEAD_DIM)
        d_normed = (jnp.einsum('te,de->td', g_q, w_q, preferred_element_type=jnp.float32)
                    + jnp.einsum('te,de->td', g_k, w_k, preferred_element_type=jnp.float32)
                    + jnp.einsum('te,de->td', g_v, w_v, preferred_element_type=jnp.float32))
        dw_q = jnp.einsum('td,te->de', normed, g_q, preferred_element_type=jnp.float32)
        dw_k = jnp.einsum('td,te->de', normed, g_k, preferred_element_type=jnp.float32)
        dw_v = jnp.einsum('td,te->de', normed, g_v, preferred_element_type=jnp.float32)
        d_hid, d_lnw = norm_vjp(d_normed)
        grad_sums = lax.psum((d_lnw, dw_q, dw_k, dw_v, dw_o), 'sp')
        return (attn_out, d_hid.astype(jnp.bfloat16), grad_sums[0].astype(jnp.bfloat16), grad_sums[1].astype(jnp.bfloat16),
                grad_sums[2].astype(jnp.bfloat16), grad_sums[3].astype(jnp.bfloat16), grad_sums[4].astype(jnp.bfloat16))

    return jax.shard_map(local_step, mesh=mesh,
                         in_specs=(row_spec, pos_spec, row_spec, P(None), full_spec, full_spec, full_spec, full_spec),
                         out_specs=(row_spec, row_spec, P('dp'), grad_spec, grad_spec, grad_spec, grad_spec),
                         check_vma=False)
```

profile of v0, /device:TPU:112, one launch (start us, length us, event | category | flops | bytes accessed | tf_op | source)
XLA Modules:
  0.0 2696.2 jit_solution(3542676681752274644)
XLA Ops:
  5.2 9.3 fusion.51
  17.0 5.8 all-to-all-start.2
  22.8 9.1 fusion.52
  34.4 11.9 fusion.62
  46.4 8.1 reshape_reshape.21
  54.5 12.9 fusion.64
  67.4 8.1 reshape_reshape.19
  77.1 5.4 all-to-all-start.4
  82.5 19.2 subtract_convert_fusion.2
  101.7 15.2 pad_maximum_fusion
  122.9 5.1 all-to-all-start
  128.1 5.2 copy.94
  136.0 30.4 %all-to-all-done = bf16[768,16,128]{0,2,1:T(8,128)(2,1)} async-done(((bf16[768,16,128]{0,2,1:T(8,128)(2,1)}), bf16[768,16,128]{0,2,1:T(8,128)(2,1)}, u32[]{:S(2)}, u32[]{:S(2)}) %all-to-all-start) | async-done | bytes 3145760 | tf_op jit(solution)/shard_map/all_to_all | solution.py:99
  166.4 4.6 all-to-all-start.1
  171.0 3.8 copy.99
  174.9 3.9 copy.106
  178.7 4.6 copy.92
  183.4 4.0 copy.100
  187.3 21.9 all-to-all-done.1
  209.2 4.6 copy.97
  216.3 1064.7 %while.26 = (s32[]{:T(128)}, f32[6144,2,128]{0,2,1:T(8,128)}, f32[6144,2,128]{0,2,1:T(8,128)}, bf16[48,128,2,1,128]{4,1,0,2,3:T(8,128)(2,1)}, bf16[48,128,2,1,12...) while((s32[]{:T(128)}, f32[6144,2,128]{0,2,1:T(8,128)}, ...), condition=%wide.region_10.11_spmd.clone, body=%wide.region_6.10_spmd.clone.sunk | while | flops 2048687488 | bytes 203239824 | solution.py:74
  240.2 3.7 fusion.131
  262.4 3.7 fusion.131
  284.5 3.7 fusion.131
  328.9 3.7 fusion.131
  351.1 3.7 fusion.131
  395.4 3.7 fusion.131
  417.6 3.7 fusion.131
  462.0 3.7 fusion.131
  506.3 3.7 fusion.131
  1281.0 7.9 copy.110
  1288.9 4.6 all-to-all-start.5
  1293.5 9.7 copy.113
  1303.2 28.5 %all-to-all-done.5 = bf16[6144,2,128]{2,1,0:T(2,128)(2,1)} async-done(((bf16[6144,2,128]{2,1,0:T(2,128)(2,1)}), bf16[6144,2,128]{2,1,0:T(2,128)(2,1)}, u32[]{:S(2)}, u32[]{:S(2)}) %all-to-all-start.5) | async-done | bytes 3145760 | tf_op jit(solution)/shard_map/all_to_all | solution.py:112
  1331.7 4.8 all-to-all-start.6
  1339.0 443.4 %while.25 = (s32[]{:T(128)}, bf16[48,128,2,1,128]{4,1,0,2,3:T(8,128)(2,1)}, s32[48]{0:T(128)S(1)}, bf16[48,128,2,1,128]{4,1,2,3,0:T(8,128)(2,1)}, bf16[6144,2,12...) while((s32[]{:T(128)}, bf16[48,128,2,1,128]{4,1,0,2,3:T(8,128)(2,1)}, ...), condition=%wide.region_5.6_spmd, body=%wide.region_2.5_spmd.sunk | while | flops 818708096 | bytes 39458972 | solution.py:52
  1782.5 7.9 copy.102
  1790.4 9.7 copy.115
  1805.7 6.6 copy.112
  1812.3 8.1 reshape.234
  1820.4 5.3 all-to-all-start.3
  1825.7 9.5 copy.114
  1835.2 8.2 reshape.235
  1843.4 19.4 subtract_convert_fusion
  1862.8 8.0 pad_maximum_fusion.3
  1870.8 7.5 convert_element_type.141
  1878.4 11.9 fusion.70
  1890.3 11.1 fusion.57
  1901.4 8.0 pad_maximum_fusion.2
  1909.5 7.5 convert_element_type.135
  1917.0 11.9 fusion.69
  1928.9 11.1 fusion.59
  1940.0 4.8 all-to-all-start.7
  1944.8 4.0 copy.103
  1948.8 4.6 copy.104
  1953.4 12.1 convolution_convert_fusion.2
  1965.5 9.6 fusion.71
  1975.1 8.1 all-to-all-done.7
  1983.2 4.0 copy.116
  1987.2 4.6 copy.117
  1991.8 13.2 fusion.55
  2005.0 17.2 fusion.48
  2022.2 4.9 fusion.66
  2029.2 666.6 %all-reduce.2 = (bf16[2048]{0:T(1024)(128)(2,1)}, bf16[2048,2048]{1,0:T(8,128)(2,1)}, bf16[2048,2048]{1,0:T(8,128)(2,1)}, bf16[2048,2048]{1,0:T(8,128)(2,1)}, bf16[2048,2048]{1,0:T(8,128)(2,1)}) all-reduce(f32[2048]{0:T(1024)S(1)} %get-tuple-element.182, f32[2048,2048]{1,0:T(8,128)} %fusion.59, ...), channel_id=1, replica_groups=mesh['dp'=2,'sp'=8] {'sp'}, use_global_device_ids=true, to_apply=%region_14.15 | all-reduce | flops 16779264 | bytes 100675584 | tf_op jit(solution)/shard_map/psum | solution.py:128
  (1793 shorter events, 1440.8 us)
Async XLA Ops:
  0.6 22.2 copy-start
  3.6 50.9 %copy-start.20 = (f32[768]{0:T(1024)}, f32[768]{0:T(1024)S(1)}, u32[]{:S(2)}) copy-start(f32[768]{0:T(1024)S(1)} %broadcast_multiply_fusion) | copy-start | bytes 9220
  5.2 49.3 %copy-start.24 = (f32[768]{0:T(1024)}, f32[768]{0:T(1024)S(1)}, u32[]{:S(2)}) copy-start(f32[768]{0:T(1024)S(1)} %fusion.54) | copy-start | bytes 9220
  5.2 49.3 %copy-start.22 = (f32[2048]{0:T(1024)}, f32[2048]{0:T(1024)S(1)}, u32[]{:S(2)}) copy-start(f32[2048]{0:T(1024)S(1)} %convert_element_type.123) | copy-start | bytes 24580
  17.0 60.1 %all-to-all-start.2 = ((bf16[768,16,128]{2,0,1:T(8,128)(2,1)}), bf16[768,16,128]{2,0,1:T(8,128)(2,1)}, u32[]{:S(2)}, u32[]{:S(2)}) async-start(bf16[768,16,128]{2,0,1:T(8,128)(2,1)} %bitcast.224), calls=%async_computation.2 | async-start | bytes 6291456 | tf_op jit(solution)/shard_map/all_to_all | solution.py:101
  77.1 45.9 %all-to-all-start.4 = ((bf16[768,16,128]{2,0,1:T(8,128)(2,1)}), bf16[768,16,128]{2,0,1:T(8,128)(2,1)}, u32[]{:S(2)}, u32[]{:S(2)}) async-start(bf16[768,16,128]{2,0,1:T(8,128)(2,1)} %bitcast.223), calls=%async_computation.4 | async-start | bytes 6291456 | tf_op jit(solution)/shard_map/all_to_all | solution.py:110
  122.9 43.4 %all-to-all-start = ((bf16[768,16,128]{0,2,1:T(8,128)(2,1)}), bf16[768,16,128]{0,2,1:T(8,128)(2,1)}, u32[]{:S(2)}, u32[]{:S(2)}) async-start(bf16[768,16,128]{0,2,1:T(8,128)(2,1)} %copy.90), calls=%async_computation | async-start | bytes 6291456 | tf_op jit(solution)/shard_map/all_to_all | solution.py:99
  166.4 42.8 %all-to-all-start.1 = ((bf16[768,16,128]{0,2,1:T(8,128)(2,1)}), bf16[768,16,128]{0,2,1:T(8,128)(2,1)}, u32[]{:S(2)}, u32[]{:S(2)}) async-start(bf16[768,16,128]{0,2,1:T(8,128)(2,1)} %copy.95), calls=%async_computation.1 | async-start | bytes 6291456 | tf_op jit(solution)/shard_map/all_to_all | solution.py:100
  244.9 9.8 slice-start
  267.1 9.8 slice-start
  289.3 9.8 slice-start
  311.5 9.8 slice-start
  333.6 9.8 slice-start
  355.8 9.8 slice-start
  378.0 9.8 slice-start
  400.2 9.8 slice-start
  422.4 9.8 slice-start
  444.5 9.8 slice-start
  466.7 9.8 slice-start
  488.9 9.8 slice-start
  533.3 9.8 slice-start
  555.5 9.8 slice-start
  577.6 9.8 slice-start
  599.8 9.8 slice-start
  622.0 9.8 slice-start
  644.2 9.8 slice-start
  666.4 9.8 slice-start
  710.7 9.8 slice-start
  732.9 9.8 slice-start
  777.3 9.8 slice-start
  799.4 9.8 slice-start
  821.6 9.8 slice-start
  843.8 9.8 slice-start
  866.0 9.8 slice-start
  888.2 9.8 slice-start
  910.3 9.8 slice-start
  954.7 9.8 slice-start
  976.9 9.8 slice-start
  999.1 9.8 slice-start
  1021.3 9.8 slice-start
  1043.4 9.8 slice-start
  1065.6 9.8 slice-start
  1087.8 9.8 slice-start
  1132.2 9.8 slice-start
  1154.3 9.8 slice-start
  1198.7 9.8 slice-start
  1220.9 9.8 slice-start
  1243.1 9.8 slice-start
  1265.2 9.8 slice-start
  1288.9 42.8 %all-to-all-start.5 = ((bf16[6144,2,128]{2,1,0:T(2,128)(2,1)}), bf16[6144,2,128]{2,1,0:T(2,128)(2,1)}, u32[]{:S(2)}, u32[]{:S(2)}) async-start(bf16[6144,2,128]{2,1,0:T(2,128)(2,1)} %copy.110), calls=%async_computation.5 | async-start | bytes 6291456 | tf_op jit(solution)/shard_map/all_to_all | solution.py:112
  1331.7 488.7 %all-to-all-start.6 = ((bf16[6144,2,128]{2,1,0:T(2,128)(2,1)}), bf16[6144,2,128]{2,1,0:T(2,128)(2,1)}, u32[]{:S(2)}, u32[]{:S(2)}) async-start(bf16[6144,2,128]{2,1,0:T(2,128)(2,1)} %copy.113), calls=%async_computation.6 | async-start | bytes 6291456 | tf_op jit(solution)/shard_map/all_to_all | solution.py:113
  1820.4 119.6 %all-to-all-start.3 = ((bf16[6144,2,128]{2,1,0:T(2,128)(2,1)}), bf16[6144,2,128]{2,1,0:T(2,128)(2,1)}, u32[]{:S(2)}, u32[]{:S(2)}) async-start(bf16[6144,2,128]{2,1,0:T(2,128)(2,1)} %copy.102), calls=%async_computation.3 | async-start | bytes 6291456 | tf_op jit(solution)/shard_map/all_to_all | solution.py:106
  1878.4 11.9 copy-start.5
  1878.4 11.9 copy-start.12
  1878.4 11.9 copy-start.21
  1878.4 11.9 copy-start.23
  1878.4 11.9 copy-start.25
  1890.3 11.1 copy-start.7
  1890.3 11.1 copy-start.8
  1917.0 11.9 copy-start.6
  1917.0 11.9 copy-start.13
  1940.0 43.2 %all-to-all-start.7 = ((bf16[6144,2,128]{2,1,0:T(2,128)(2,1)}), bf16[6144,2,128]{2,1,0:T(2,128)(2,1)}, u32[]{:S(2)}, u32[]{:S(2)}) async-start(bf16[6144,2,128]{2,1,0:T(2,128)(2,1)} %copy.115), calls=%async_computation.7 | async-start | bytes 6291456 | tf_op jit(solution)/shard_map/all_to_all | solution.py:114
  1953.4 12.1 copy-start.14
  2005.0 17.2 copy-start.19
  (399 other events, 1507.3 us)
where the time goes:
time: 2710 us; the launch traced here: 2700 us
  matrix products  1110 us (41%)
  blocking collectives  667 us (25%)
  local copies, waits for them, and re-layouts  397 us (15%)
  other arithmetic  323 us (12%)
  waiting for transfers between devices  88.9 us (3%)
  loops' own time  66.5 us (2%)
  starting transfers between devices  40.6 us (1%)
    psum x1, blocking collectives, local_step(): grad_sums = lax.psum((d_lnw, dw_q, dw_k, dw_v, dw_o), 'sp')  667 us
    dot_general x96, matrix products, block_probs(): jnp.einsum('qgrd,kgd->grqk', q_block, k_all, preferred_element_type=jnp.f...  342 us
    while x864, local copies, waits for them, and re-layouts  177 us
    dot_general x48, matrix products, one_block(): jnp.einsum('grqk,qgrd->kgd', attn_prob.astype(jnp.bfloat16), do_block, pr...  157 us
    dot_general x48, matrix products, one_block(): jnp.einsum('grqk,qgrd->kgd', d_score, q_block, preferred_element_type=jnp...  155 us
    dot_general x48, matrix products, one_block(): jnp.einsum('qgrd,kgd->grqk', do_block, v_all, preferred_element_type=jnp....  134 us
    another operation x50, other arithmetic  130 us
    dot_general x48, matrix products, one_block(): jnp.einsum('grqk,kgd->qgrd', attn_prob.astype(jnp.bfloat16), v_all, prefe...  103 us
  transfers between devices with their start and end apart: 8, of which 4 were waited for; matrix products, arithmetic and copies ran while one was open for 25% of the time, Pallas kernels for 0%

commit v1 on v0

v1 whole, which is shorter than its diff:
```python
import functools
import math
import jax
import jax.numpy as jnp
from jax import lax
from jax.experimental import pallas as pl
from jax.experimental.pallas import tpu as pltpu
from jax.sharding import PartitionSpec as P

HEAD_DIM = 128
LN_EPS = 1e-5
ROPE_BASE = 10000.0
SCALE = HEAD_DIM ** -0.5
EXP2_SCALE = SCALE * math.log2(math.e)
BLOCK = 512
VMEM_LIMIT = 56 * 1024 * 1024
LAST = (((1,), (1,)), ((), ()))
PLAIN = (((1,), (0,)), ((), ()))


def norm_f32(hid_f32, weight_f32):
    mean_val = jnp.mean(hid_f32, axis=-1, keepdims=True)
    centered = hid_f32 - mean_val
    var_val = jnp.mean(centered * centered, axis=-1, keepdims=True)
    return centered * lax.rsqrt(var_val + LN_EPS) * weight_f32


def rope_tables(positions):
    inv_freq = ROPE_BASE ** (-jnp.arange(0, HEAD_DIM, 2, dtype=jnp.float32) / HEAD_DIM)
    angles = positions.astype(jnp.float32)[:, None] * inv_freq[None, :]
    cos_t, sin_t = jnp.cos(angles), jnp.sin(angles)
    cos_full = jnp.stack([cos_t, cos_t], axis=-1).reshape(-1, HEAD_DIM)
    sin_full = jnp.stack([-sin_t, sin_t], axis=-1).reshape(-1, HEAD_DIM)
    return cos_full, sin_full


def swap_pairs(x):
    lane = lax.broadcasted_iota(jnp.int32, x.shape, 1)
    up = pltpu.roll(x, HEAD_DIM - 1, 1)
    down = pltpu.roll(x, 1, 1)
    return jnp.where(lane % 2 == 0, up, down)


def dot_f32(a, b, dims):
    return lax.dot_general(a, b, dims, preferred_element_type=jnp.float32)


def proj_kernel(h_ref, wq_ref, wk_ref, wv_ref, cos_ref, sin_ref, q_ref, k_ref, v_ref, kt_ref, vt_ref):
    h = h_ref[...]
    cos_t, sin_t = cos_ref[...], sin_ref[...]
    q = dot_f32(h, wq_ref[...], PLAIN)
    k = dot_f32(h, wk_ref[...], PLAIN)
    v = dot_f32(h, wv_ref[...], PLAIN)
    for n in range(q.shape[1] // HEAD_DIM):
        cols = slice(n * HEAD_DIM, (n + 1) * HEAD_DIM)
        qn, kn, vn = q[:, cols], k[:, cols], v[:, cols]
        q_ref[:, cols] = (qn * cos_t + swap_pairs(qn) * sin_t).astype(jnp.bfloat16)
        kn = kn * cos_t + swap_pairs(kn) * sin_t
        k_ref[:, cols] = kn.astype(jnp.bfloat16)
        v_ref[:, cols] = vn.astype(jnp.bfloat16)
        kt_ref[cols, :] = kn.T.astype(jnp.bfloat16)
        vt_ref[cols, :] = vn.T.astype(jnp.bfloat16)


def project(h_all, w_q, w_k, w_v, cos_full, sin_full):
    rows, depth = h_all.shape
    cols = w_q.shape[1]
    tile = BLOCK
    row_spec = lambda width: pl.BlockSpec((tile, width), lambda i: (i, 0))
    full = pl.BlockSpec((depth, cols), lambda i: (0, 0))
    col_spec = pl.BlockSpec((cols, tile), lambda i: (0, i))
    out = jax.ShapeDtypeStruct((rows, cols), jnp.bfloat16)
    out_t = jax.ShapeDtypeStruct((cols, rows), jnp.bfloat16)
    return pl.pallas_call(
        proj_kernel, grid=(rows // tile,),
        in_specs=[row_spec(depth), full, full, full, row_spec(HEAD_DIM), row_spec(HEAD_DIM)],
        out_specs=[row_spec(cols)] * 3 + [col_spec] * 2,
        out_shape=[out] * 3 + [out_t] * 2,
        compiler_params=pltpu.CompilerParams(vmem_limit_bytes=VMEM_LIMIT),
        cost_estimate=pl.CostEstimate(flops=6 * rows * depth * cols, bytes_accessed=2 * rows * (depth + 5 * cols), transcendentals=0),
        name="project",
    )(h_all, w_q, w_k, w_v, cos_full, sin_full)


def causal(st, key_start, q_start):
    keys = lax.broadcasted_iota(jnp.int32, st.shape, 0) + key_start
    qs = lax.broadcasted_iota(jnp.int32, st.shape, 1) + q_start
    return jnp.where(keys <= qs, st, -jnp.inf)


def fwd_kernel(q_ref, k_ref, vt_ref, o_ref, ot_ref, lse_ref, acc_ref):
    i = pl.program_id(1)
    q = q_ref[...]
    acc_ref[...] = jnp.zeros_like(acc_ref)

    def step(j, carry, masked):
        m, l = carry
        start = pl.multiple_of(j * BLOCK, BLOCK)
        st = dot_f32(k_ref[pl.ds(start, BLOCK), :], q, LAST)
        if masked:
            st = causal(st, 0, 0)
        m_new = jnp.maximum(m, jnp.max(st, axis=0, keepdims=True))
        p = jnp.exp2((st - m_new) * EXP2_SCALE)
        alpha = jnp.exp2((m - m_new) * EXP2_SCALE)
        l = l * alpha + jnp.sum(p, axis=0, keepdims=True)
        acc_ref[...] = acc_ref[...] * alpha + dot_f32(vt_ref[:, pl.ds(start, BLOCK)], p.astype(jnp.bfloat16), PLAIN)
        return m_new, l

    init = (jnp.full((1, q.shape[0]), -jnp.inf, jnp.float32), jnp.zeros((1, q.shape[0]), jnp.float32))
    carry = lax.fori_loop(0, i, lambda j, c: step(j, c, False), init)
    m, l = step(i, carry, True)
    ot = acc_ref[...] / l
    ot_ref[...] = ot
    o_ref[...] = ot.T.astype(jnp.bfloat16)
    lse_ref[0] = m * EXP2_SCALE + jnp.log2(l)


def attn_forward(q, k, vt):
    rows, cols = q.shape
    heads = cols // HEAD_DIM
    blocks = rows // BLOCK
    flops = 2 * 2 * rows * rows * cols // 2
    return pl.pallas_call(
        fwd_kernel, grid=(heads, blocks),
        in_specs=[pl.BlockSpec((BLOCK, HEAD_DIM), lambda h, i: (i, h)),
                  pl.BlockSpec((rows, HEAD_DIM), lambda h, i: (0, h)),
                  pl.BlockSpec((HEAD_DIM, rows), lambda h, i: (h, 0))],
        out_specs=[pl.BlockSpec((BLOCK, HEAD_DIM), lambda h, i: (i, h)),
                   pl.BlockSpec((HEAD_DIM, BLOCK), lambda h, i: (h, i)),
                   pl.BlockSpec((1, 1, BLOCK), lambda h, i: (h, 0, i))],
        out_shape=[jax.ShapeDtypeStruct((rows, cols), jnp.bfloat16),
                   jax.ShapeDtypeStruct((cols, rows), jnp.float32),
                   jax.ShapeDtypeStruct((heads, 1, rows), jnp.float32)],
        scratch_shapes=[pltpu.VMEM((HEAD_DIM, BLOCK), jnp.float32)],
        compiler_params=pltpu.CompilerParams(vmem_limit_bytes=VMEM_LIMIT),
        cost_estimate=pl.CostEstimate(flops=2 * flops, bytes_accessed=10 * rows * cols, transcendentals=0),
        name="attn_fwd",
    )(q, k, vt)


def unrope(x, cos_t, sin_t):
    x = x.astype(jnp.bfloat16).astype(jnp.float32)
    return (x * cos_t - swap_pairs(x) * sin_t).astype(jnp.bfloat16)


def bwd_kernel(q_ref, do_ref, ot_ref, lse_ref, k_ref, v_ref, kt_ref, cos_ref, sin_ref,
               gq_ref, gk_ref, gv_ref, dk_acc, dv_acc, dqt_acc):
    i = pl.program_id(1)

    @pl.when(i == 0)
    def _():
        dk_acc[...] = jnp.zeros_like(dk_acc)
        dv_acc[...] = jnp.zeros_like(dv_acc)

    q = q_ref[...]
    do = do_ref[...]
    lse = lse_ref[0]
    row_dot = jnp.sum(do.astype(jnp.float32).T * ot_ref[...], axis=0, keepdims=True)
    dqt_acc[...] = jnp.zeros_like(dqt_acc)

    def step(j, masked):
        start = pl.multiple_of(j * BLOCK, BLOCK)
        rows = pl.ds(start, BLOCK)
        st = dot_f32(k_ref[rows, :], q, LAST)
        dpt = dot_f32(v_ref[rows, :], do, LAST)
        if masked:
            st = causal(st, 0, 0)
        p = jnp.exp2(st * EXP2_SCALE - lse)
        ds = (p * (dpt - row_dot) * SCALE).astype(jnp.bfloat16)
        dv_acc[rows, :] += dot_f32(p.astype(jnp.bfloat16), do, PLAIN)
        dk_acc[rows, :] += dot_f32(ds, q, PLAIN)
        dqt_acc[...] += dot_f32(kt_ref[:, rows], ds, PLAIN)

    lax.fori_loop(0, i, lambda j, c: (step(j, False), c)[1], 0)
    step(i, True)
    tile = pl.ds(pl.multiple_of(i * BLOCK, BLOCK), BLOCK)
    gq_ref[...] = unrope(dqt_acc[...].T, cos_ref[tile, :], sin_ref[tile, :])

    @pl.when(i == pl.num_programs(1) - 1)
    def _():
        def finish(j, c):
            rows = pl.ds(pl.multiple_of(j * BLOCK, BLOCK), BLOCK)
            gk_ref[rows, :] = unrope(dk_acc[rows, :], cos_ref[rows, :], sin_ref[rows, :])
            gv_ref[rows, :] = dv_acc[rows, :].astype(jnp.bfloat16)
            return c
        lax.fori_loop(0, dk_acc.shape[0] // BLOCK, finish, 0)


def attn_backward(q, do, ot, lse, k, v, kt, cos_full, sin_full):
    rows, cols = q.shape
    heads = cols // HEAD_DIM
    flops = 2 * rows * rows * cols // 2
    q_spec = pl.BlockSpec((BLOCK, HEAD_DIM), lambda h, i: (i, h))
    all_spec = pl.BlockSpec((rows, HEAD_DIM), lambda h, i: (0, h))
    table = pl.BlockSpec((rows, HEAD_DIM), lambda h, i: (0, 0))
    out = jax.ShapeDtypeStruct((rows, cols), jnp.bfloat16)
    return pl.pallas_call(
        bwd_kernel, grid=(heads, rows // BLOCK),
        in_specs=[q_spec, q_spec,
                  pl.BlockSpec((HEAD_DIM, BLOCK), lambda h, i: (h, i)),
                  pl.BlockSpec((1, 1, BLOCK), lambda h, i: (h, 0, i)),
                  all_spec, all_spec,
                  pl.BlockSpec((HEAD_DIM, rows), lambda h, i: (h, 0)),
                  table, table],
        out_specs=[q_spec, all_spec, all_spec],
        out_shape=[out] * 3,
        scratch_shapes=[pltpu.VMEM((rows, HEAD_DIM), jnp.float32),
                        pltpu.VMEM((rows, HEAD_DIM), jnp.float32),
                        pltpu.VMEM((HEAD_DIM, BLOCK), jnp.float32)],
        compiler_params=pltpu.CompilerParams(vmem_limit_bytes=VMEM_LIMIT),
        cost_estimate=pl.CostEstimate(flops=5 * flops, bytes_accessed=20 * rows * cols, transcendentals=0),
        name="attn_bwd",
    )(q, do, ot, lse, k, v, kt, cos_full, sin_full)


def solution(mesh):
    sp_size = mesh.shape['sp']
    row_spec = P(('dp', 'sp'), None)
    pos_spec = P(('dp', 'sp'))
    full_spec = P(None, None)
    grad_spec = P('dp', None)

    def local_step(hidden, positions, d_attn, ln_weight, w_q, w_k, w_v, w_o):
        me = lax.axis_index('sp')
        cols = w_q.shape[1] // sp_size
        normed32, norm_vjp = jax.vjp(norm_f32, hidden.astype(jnp.float32), ln_weight.astype(jnp.float32))
        normed = normed32.astype(jnp.bfloat16)
        pos_all = lax.all_gather(positions, 'sp', tiled=True)
        h_all = lax.all_gather(normed, 'sp', tiled=True)
        g_all = lax.all_gather(d_attn, 'sp', tiled=True)
        cos_full, sin_full = rope_tables(pos_all)
        mine = lambda w, axis: lax.dynamic_slice_in_dim(w, me * cols, cols, axis)
        wq_my, wk_my, wv_my, wo_my = mine(w_q, 1), mine(w_k, 1), mine(w_v, 1), mine(w_o, 0)
        q, k, v, kt, vt = project(h_all, wq_my, wk_my, wv_my, cos_full, sin_full)
        o, ot, lse = attn_forward(q, k, vt)
        o_tok = lax.all_to_all(o, 'sp', 0, 1, tiled=True)
        d_o = jnp.einsum('td,ed->te', g_all, wo_my, preferred_element_type=jnp.float32).astype(jnp.bfloat16)
        dwo_my = jnp.einsum('te,td->ed', o, g_all, preferred_element_type=jnp.float32).astype(jnp.bfloat16)
        gq, gk, gv = attn_backward(q, d_o, ot, lse, k, v, kt, cos_full, sin_full)
        dw_o = lax.all_gather(dwo_my, 'sp', tiled=True)
        to_tok = lambda x: lax.all_to_all(x, 'sp', 0, 1, tiled=True)
        gq_tok, gk_tok, gv_tok = to_tok(gq), to_tok(gk), to_tok(gv)
        wgrad = lambda x: jnp.einsum('td,te->de', h_all, x, preferred_element_type=jnp.float32).astype(jnp.bfloat16)
        gather = lambda x: lax.all_gather(x, 'sp', axis=1, tiled=True)
        dw_q, dw_k, dw_v = gather(wgrad(gq)), gather(wgrad(gk)), gather(wgrad(gv))
        attn_out = jnp.dot(o_tok, w_o, preferred_element_type=jnp.float32).astype(jnp.bfloat16)
        d_normed = (jnp.einsum('te,de->td', gq_tok, w_q, preferred_element_type=jnp.float32)
                    + jnp.einsum('te,de->td', gk_tok, w_k, preferred_element_type=jnp.float32)
                    + jnp.einsum('te,de->td', gv_tok, w_v, preferred_element_type=jnp.float32))
        d_hid, d_lnw = norm_vjp(d_normed)
        d_lnw = lax.psum(d_lnw, 'sp')
        return (attn_out, d_hid.astype(jnp.bfloat16), d_lnw.astype(jnp.bfloat16), dw_q, dw_k, dw_v, dw_o)

    return jax.shard_map(local_step, mesh=mesh,
                         in_specs=(row_spec, pos_spec, row_spec, P(None), full_spec, full_spec, full_spec, full_spec),
                         out_specs=(row_spec, row_spec, P('dp'), grad_spec, grad_spec, grad_spec, grad_spec),
                         check_vma=False)
```

time: 2710 us -> 798 us (0.29)
  matrix products: 1110 us -> 120 us
  blocking collectives: 667 us -> 54.5 us
  local copies, waits for them, and re-layouts: 397 us -> 76.5 us
  other arithmetic: 323 us -> 21.9 us
  Pallas kernels: 0 us -> 288 us
  waiting for transfers between devices: 88.9 us -> 199 us
  loops' own time: 66.5 us -> 0 us
    dot_general x347 -> x8, matrix products: 1100 us -> 108 us  [the longest x3 40.1 us: local_step(): jnp.einsum('td,te->de', h_all, x, preferred_element_type=jnp.float32)]
    psum x1, blocking collectives: 667 us -> 29.8 us  [local_step(): d_lnw = lax.psum(d_lnw, 'sp')]
    pallas_call x0 -> x3, Pallas kernels: none -> 288 us  [the longest x1 146 us: attn_backward(): pl.pallas_call(bwd_kernel, grid=(heads, rows // BLOCK), in_specs=[q_spec,...]
    while x867 -> x0, local copies, waits for them, and re-layouts: 200 us -> none
    another operation x53 -> x1, other arithmetic: 161 us -> 2.14 us  [rope_tables(): cos_full = jnp.stack([cos_t, cos_t], axis=-1).reshape(-1, HEAD_DIM)]
    reduce_sum x96 -> x0, other arithmetic: 97.4 us -> none  [block_probs(): return jax.nn.softmax(scores, axis=-1)]
    another operation x2 -> x0, loops' own time: 66.5 us -> none  [the longest x1 34 us: attn_backward(): lax.scan(one_block, (zero_acc, zero_acc), (q_grp.reshape(block_shape), do...]
    all_gather x0 -> x6, waiting for transfers between devices: none -> 60.8 us  [the longest x1 60.7 us: local_step(): h_all = lax.all_gather(normed, 'sp', tiled=True)]
  transfers between devices with their start and end apart: 8 -> 10, of which waited for: 4 -> 4; matrix products, arithmetic and copies ran while one was open for 25% -> 20% of each run, Pallas kernels for 0% -> 36%
where the time goes in v1:
time: 798 us; the launch traced here: 794 us
  Pallas kernels  288 us (36%)
  waiting for transfers between devices  199 us (25%)
  matrix products  120 us (15%)
  local copies, waits for them, and re-layouts  76.5 us (10%)
  blocking collectives  54.5 us (7%)
  other arithmetic  21.9 us (3%)
  starting transfers between devices  19.8 us (2%)
  between operations  14.7 us (2%)
    pallas_call x1, Pallas kernels, attn_backward(): pl.pallas_call(bwd_kernel, grid=(heads, rows // BLOCK), in_specs=[q_spec,...  146 us
    all_to_all x3, waiting for transfers between devices, local_step(): to_tok = lambda x: lax.all_to_all(x, 'sp', 0, 1, tiled=True)  137 us
    pallas_call x1, Pallas kernels, attn_forward(): pl.pallas_call(fwd_kernel, grid=(heads, blocks), in_specs=[pl.BlockSpec((...  111 us
    all_gather x1, waiting for transfers between devices, local_step(): h_all = lax.all_gather(normed, 'sp', tiled=True)  60.7 us
    dot_general x3, matrix products, local_step(): jnp.einsum('td,te->de', h_all, x, preferred_element_type=jnp.float32)  40.1 us
    unnamed x35, local copies, waits for them, and re-layouts  35.6 us
    pallas_call x1, Pallas kernels, project(): pl.pallas_call(proj_kernel, grid=(rows // tile,), in_specs=[row_spec(dept...  30.4 us
    psum x1, blocking collectives, local_step(): d_lnw = lax.psum(d_lnw, 'sp')  29.8 us
  transfers between devices with their start and end apart: 10, of which 4 were waited for; matrix products, arithmetic and copies ran while one was open for 20% of the time, Pallas kernels for 36%

profile of v1, /device:TPU:112, one launch (start us, length us, event | category | flops | bytes accessed | tf_op | source)
XLA Modules:
  0.0 794.3 jit_solution(497104333591786361)
XLA Ops:
  7.2 0.0 copy-start
  7.2 0.1 all-gather.8.cloned.1.call-start
  7.3 2.5 convert_reduce_fusion
  9.8 2.8 fusion.9
  12.7 0.6 copy-done.9
  13.3 0.6 copy-done.11
  13.9 0.6 copy-done.5
  14.5 2.7 fusion.7
  17.1 0.1 all-gather.8.cloned.1.call-update
  17.2 0.1 all-gather.10.cloned.1.call-start
  17.2 0.7 all-gather.10.cloned.1.call-update
  18.0 0.1 all-gather.18.cloned.1.call-start
  18.1 24.7 %all-gather = s32[8,1,768]{2,1,0:T(1,128)S(1)} all-gather(s32[1,1,768]{2,1,0:T(1,128)S(1)} %reshape.200), channel_id=1, replica_groups=mesh['dp'=2,'sp'=8] {'sp'}, dimensions={0}, use_global_device_ids=true | all-gather | bytes 27648 | tf_op jit(solution)/shard_map/all_gather | solution.py:228
  42.8 5.5 fusion.12
  48.4 2.1 pad_maximum_fusion
  50.5 2.4 copy.34
  52.9 3.5 reshape.198
  56.5 3.5 copy.36.cos_ref
  60.0 4.3 copy.35
  64.3 3.3 reshape.199
  67.7 3.5 copy.37.sin_ref
  71.2 2.3 constant_dynamic-slice_fusion.2.wq_ref
  73.5 3.0 constant_dynamic-slice_fusion
  76.5 60.7 %all-gather.8.cloned.1.call-done.h_ref = bf16[6144,2048]{1,0:T(8,128)(2,1)} async-done(((bf16[768,2048]{1,0:T(8,128)(2,1)}), bf16[6144,2048]{1,0:T(8,128)(2,1)}) %all-gather.8.cloned.1.call-update) | async-done | bytes 25165840 | tf_op jit(solution)/shard_map/all_gather | solution.py:229
  137.2 30.4 %project.1 = (bf16[6144,256]{1,0:T(8,128)(2,1)}, bf16[6144,256]{1,0:T(8,128)(2,1)}, bf16[6144,256]{1,0:T(8,128)(2,1)}, bf16[256,6144]{1,0:T(8,128)(2,1)}, bf16[256,6144]{1,0:T(8,128)(2,1)}) custom-call(bf16[6144,2048]{1,0:T(8,128)(2,1)} %all-gather.8.cloned.1.call-done.h_ref, bf16[2048,256]{1,0:T(8,128)(2,1)} %constant_dynamic-slice_fusion.2.wq_ref, ...), custom_call_target="tpu_custom_call" | custom-call | flops 19327352832 | bytes 40894464 | tf_op jit(solution)/shard_map/project/pallas_call | solution.py:74
  167.7 111.4 %attn_fwd.1 = (bf16[6144,256]{1,0:T(8,128)(2,1)}, f32[256,6144]{1,0:T(8,128)}, f32[2,1,6144]{2,1,0:T(1,128)}) custom-call(bf16[6144,256]{1,0:T(8,128)(2,1)} %get-tuple-element.18.q_ref, bf16[6144,256]{1,0:T(8,128)(2,1)} %get-tuple-element.19.k_ref, bf16[256,6144]{1,0:T(8,128)(2,1)} %get-tuple-element.20.vt_ref), custom_call_target="tpu_custom_call" | custom-call | flops 38654705664 | bytes 15728640 | tf_op jit(solution)/shard_map/attn_fwd/pallas_call | solution.py:123
  279.1 13.4 %convolution_convert_fusion.5 = bf16[256,2048]{1,0:T(8,128)(2,1)} fusion(bf16[6144,256]{1,0:T(8,128)(2,1)} %get-tuple-element.21, bf16[6144,2048]{1,0:T(8,128)(2,1)} %all-gather.10.cloned.1.call-done), kind=kOutput, calls=%fused_computation.23 | convolution fusion | flops 6442975232 | bytes 29360128 | tf_op jit(solution)/shard_map/te,td->ed/dot_general | solution.py:238
  292.4 0.1 all-gather.18.cloned.1.call-update
  292.5 0.1 all-gather.12.cloned.1.call-start
  292.6 13.5 %fusion.4.do_ref = bf16[6144,256]{1,0:T(8,128)(2,1)} fusion(bf16[6144,2048]{1,0:T(8,128)(2,1)} %all-gather.10.cloned.1.call-done, bf16[2048,2048]{1,0:T(8,128)(2,1)} %param.15, s32[]{:T(128)S(6)} %select_n.2), kind=kOutput, calls=%fused_computation.8 | convolution fusion | flops 6444023808 | bytes 29360132 | tf_op jit(solution)/shard_map/td,ed->te/dot_general | solution.py:237
  306.1 146.3 %attn_bwd.1 = (bf16[6144,256]{1,0:T(8,128)(2,1)}, bf16[6144,256]{1,0:T(8,128)(2,1)}, bf16[6144,256]{1,0:T(8,128)(2,1)}) custom-call(bf16[6144,256]{1,0:T(8,128)(2,1)} %get-tuple-element.18.q_ref, bf16[6144,256]{1,0:T(8,128)(2,1)} %fusion.4.do_ref, f32[256,6144]{1,0:T(8,128)} %get-tuple-element.22.ot_ref, f32[2,1,6144]{2,1,0:T(1,128)} %get-tuple-element.23.lse_ref, ...), custom_call_target="tpu_custom_call" | custom-call | flops 48318382080 | bytes 31457280 | tf_op jit(solution)/shard_map/attn_bwd/pallas_call | solution.py:197
  452.4 13.5 %convolution_convert_fusion.4 = bf16[2048,256]{1,0:T(8,128)(2,1)} fusion(bf16[6144,2048]{1,0:T(8,128)(2,1)} %all-gather.8.cloned.1.call-done.h_ref, bf16[6144,256]{1,0:T(8,128)(2,1)} %get-tuple-element.26), kind=kOutput, calls=%fused_computation.22 | convolution fusion | flops 6442975232 | bytes 29360128 | tf_op jit(solution)/shard_map/td,te->de/dot_general | solution.py:243
  465.8 0.1 all-gather.12.cloned.1.call-update
  465.9 0.1 all-gather.16.cloned.1.call-start
  466.0 13.3 %convolution_convert_fusion.2 = bf16[2048,256]{1,0:T(8,128)(2,1)} fusion(bf16[6144,2048]{1,0:T(8,128)(2,1)} %all-gather.8.cloned.1.call-done.h_ref, bf16[6144,256]{1,0:T(8,128)(2,1)S(1)} %copy-done.3), kind=kOutput, calls=%fused_computation.20 | convolution fusion | flops 6442975232 | bytes 29360128 | tf_op jit(solution)/shard_map/td,te->de/dot_general | solution.py:243
  479.3 0.1 all-gather.16.cloned.1.call-update
  479.3 0.1 all-gather.14.cloned.1.call-start
  479.4 13.3 %convolution_convert_fusion.3 = bf16[2048,256]{1,0:T(8,128)(2,1)} fusion(bf16[6144,2048]{1,0:T(8,128)(2,1)} %all-gather.8.cloned.1.call-done.h_ref, bf16[6144,256]{1,0:T(8,128)(2,1)} %get-tuple-element.27), kind=kOutput, calls=%fused_computation.21 | convolution fusion | flops 6442975232 | bytes 29360128 | tf_op jit(solution)/shard_map/td,te->de/dot_general | solution.py:243
  492.7 0.1 all-gather.14.cloned.1.call-update
  492.8 4.8 copy.43
  497.6 4.6 all-to-all-start.2
  502.2 2.8 copy.42
  505.0 47.1 %all-to-all-done.2 = bf16[8,768,256]{1,2,0:T(8,128)(2,1)} async-done(((bf16[8,768,256]{1,2,0:T(8,128)(2,1)}), bf16[8,768,256]{1,2,0:T(8,128)(2,1)}, u32[]{:S(2)}, u32[]{:S(2)}) %all-to-all-start.2) | async-done | bytes 3145760 | tf_op jit(solution)/shard_map/all_to_all | solution.py:241
  552.1 5.3 all-to-all-start.1
  557.4 4.6 copy.44
  562.1 2.8 copy.38
  564.8 53.4 %all-to-all-done.1 = bf16[8,768,256]{1,2,0:T(8,128)(2,1)} async-done(((bf16[8,768,256]{1,2,0:T(8,128)(2,1)}), bf16[8,768,256]{1,2,0:T(8,128)(2,1)}, u32[]{:S(2)}, u32[]{:S(2)}) %all-to-all-start.1) | async-done | bytes 3145760 | tf_op jit(solution)/shard_map/all_to_all | solution.py:241
  618.2 4.8 all-to-all-start.3
  623.0 11.8 %fusion.17 = f32[768,2048]{1,0:T(8,128)} fusion(bf16[768,2048]{0,1:T(8,128)(2,1)} %bitcast.10, bf16[2048,2048]{1,0:T(8,128)(2,1)} %param.13), kind=kOutput, calls=%fused_computation.40 | convolution fusion | flops 6442450944 | bytes 17825792 | tf_op jit(solution)/shard_map/te,de->td/dot_general | solution.py:248
  634.8 11.8 %fusion.16 = f32[768,2048]{1,0:T(8,128)} fusion(bf16[768,2048]{0,1:T(8,128)(2,1)} %bitcast.7, bf16[2048,2048]{1,0:T(8,128)(2,1)} %param.12), kind=kOutput, calls=%fused_computation.39 | convolution fusion | flops 6442450944 | bytes 17825792 | tf_op jit(solution)/shard_map/te,de->td/dot_general | solution.py:247
  646.6 0.0 copy-start.12
  646.6 37.0 %all-to-all-done.3 = bf16[8,768,256]{1,2,0:T(8,128)(2,1)} async-done(((bf16[8,768,256]{1,2,0:T(8,128)(2,1)}), bf16[8,768,256]{1,2,0:T(8,128)(2,1)}, u32[]{:S(2)}, u32[]{:S(2)}) %all-to-all-start.3) | async-done | bytes 3145760 | tf_op jit(solution)/shard_map/all_to_all | solution.py:241
  683.6 4.6 all-to-all-start
  688.3 17.1 %fusion.8 = (f32[2048]{0:T(1024)S(1)}, f32[768]{0:T(1024)S(1)}, f32[768,2048]{1,0:T(8,128)}) fusion(bf16[768,2048]{1,0:T(8,128)(2,1)S(1)} %copy-done.1, f32[768]{0:T(1024)S(1)} %copy-done.12, f32[768]{0:T(1024)S(1)} %copy-done.8, f32[2048]{0:T(1024)S(1)} %copy-done.6, bf16[768,2048]{0,1:T(8,128)(2,1)} %bitcast.13, bf16[2048,2048]{1,0:T(8,128)(2,1)} %param.14, ...), kind=kOutput, calls=%fused_computation.12 | convolution fusion | flops 6458176512 | bytes 33580032 | tf_op jit(solution)/shard_map/te,de->td/dot_general | solution.py:249
  705.4 29.8 %psum.7 = bf16[2048]{0:T(1024)(128)(2,1)} all-reduce(f32[2048]{0:T(1024)S(1)} %get-tuple-element.29), channel_id=1, replica_groups=mesh['dp'=2,'sp'=8] {'sp'}, use_global_device_ids=true, to_apply=%region_5.0 | all-reduce | flops 2048 | bytes 12288 | tf_op jit(solution)/shard_map/psum | solution.py:251
  735.2 4.1 fusion.15
  739.3 2.1 add_convert_fusion
  741.4 0.0 all-to-all-done
  741.4 12.0 %convolution_convert_fusion.1 = bf16[768,2048]{1,0:T(8,128)(2,1)} fusion(bf16[768,2048]{0,1:T(8,128)(2,1)} %bitcast.3, bf16[2048,2048]{1,0:T(8,128)(2,1)} %param.15), kind=kOutput, calls=%fused_computation.17 | convolution fusion | flops 6444023808 | bytes 14680064 | tf_op jit(solution)/shard_map/dot_general | solution.py:246
  753.3 0.0 all-gather.14.cloned.1.call-done
  753.4 8.4 %copy.50 = bf16[2048,2048]{1,0:T(8,128)(2,1)} copy(bf16[2048,2048]{1,0:T(8,128)(2,1)} %all-gather.12.cloned.1.call-done) | data formatting | bytes 16777216
  761.8 8.4 %copy.51 = bf16[2048,2048]{1,0:T(8,128)(2,1)} copy(bf16[2048,2048]{1,0:T(8,128)(2,1)} %all-gather.14.cloned.1.call-done) | data formatting | bytes 16777216
  770.3 8.4 %copy.52 = bf16[2048,2048]{1,0:T(8,128)(2,1)} copy(bf16[2048,2048]{1,0:T(8,128)(2,1)} %all-gather.16.cloned.1.call-done) | data formatting | bytes 16777216
  778.7 8.4 %copy.53 = bf16[2048,2048]{1,0:T(8,128)(2,1)} copy(bf16[2048,2048]{1,0:T(8,128)(2,1)} %all-gather.18.cloned.1.call-done) | data formatting | bytes 16777216
  (37 shorter events, 0.1 us)
Async XLA Ops:
  7.2 7.3 copy-start
  7.2 6.1 copy-start.13
  7.2 130.0 %all-gather.8.cloned.1.call-start = ((), (), s32[]{:S(2)}) async-start(), calls=%async_computation.4 | async-start | bytes 28311552 | tf_op jit(solution)/shard_map/all_gather | solution.py:229
  9.8 3.5 copy-start.7
  12.7 0.6 copy-start.9
  13.3 0.6 copy-start.11
  13.9 0.6 copy-start.5
  14.5 3.6 copy-start.14
  17.2 261.9 %all-gather.10.cloned.1.call-start = ((), (), s32[]{:S(2)}) async-start(), calls=%async_computation.5 | async-start | bytes 28311552 | tf_op jit(solution)/shard_map/all_gather | solution.py:230
  18.0 735.4 %all-gather.18.cloned.1.call-start = ((), (), s32[]{:S(2)}) async-start(), calls=%async_computation.9 | async-start | bytes 9437184 | tf_op jit(solution)/shard_map/all_gather | solution.py:240
  292.5 460.9 %all-gather.12.cloned.1.call-start = ((), (), s32[]{:S(2)}) async-start(), calls=%async_computation.6 | async-start | bytes 9437184 | tf_op jit(solution)/shard_map/all_gather | solution.py:244
  452.4 13.6 %copy-start.3 = (bf16[6144,256]{1,0:T(8,128)(2,1)S(1)}, bf16[6144,256]{1,0:T(8,128)(2,1)}, u32[]{:S(2)}) copy-start(bf16[6144,256]{1,0:T(8,128)(2,1)} %get-tuple-element.28) | copy-start | bytes 9437188
  465.9 287.4 %all-gather.16.cloned.1.call-start = ((), (), s32[]{:S(2)}) async-start(), calls=%async_computation.8 | async-start | bytes 9437184 | tf_op jit(solution)/shard_map/all_gather | solution.py:244
  479.3 274.0 %all-gather.14.cloned.1.call-start = ((), (), s32[]{:S(2)}) async-start(), calls=%async_computation.7 | async-start | bytes 9437184 | tf_op jit(solution)/shard_map/all_gather | solution.py:244
  492.8 9.4 %copy-start.4 = (bf16[6144,256]{1,0:T(8,128)(2,1)S(1)}, bf16[6144,256]{1,0:T(8,128)(2,1)}, u32[]{:S(2)}) copy-start(bf16[6144,256]{1,0:T(8,128)(2,1)} %get-tuple-element.26) | copy-start | bytes 9437188
  497.6 54.5 %all-to-all-start.2 = ((bf16[8,768,256]{1,2,0:T(8,128)(2,1)}), bf16[8,768,256]{1,2,0:T(8,128)(2,1)}, u32[]{:S(2)}, u32[]{:S(2)}) async-start(bf16[8,768,256]{1,2,0:T(8,128)(2,1)} %copy.43), calls=%async_computation.2 | async-start | bytes 6291456 | tf_op jit(solution)/shard_map/all_to_all | solution.py:241
  505.0 57.0 %copy-start.2 = (bf16[6144,256]{1,0:T(8,128)(2,1)S(1)}, bf16[6144,256]{1,0:T(8,128)(2,1)}, u32[]{:S(2)}) copy-start(bf16[6144,256]{1,0:T(8,128)(2,1)} %get-tuple-element.21) | copy-start | bytes 9437188
  552.1 66.1 %all-to-all-start.1 = ((bf16[8,768,256]{1,2,0:T(8,128)(2,1)}), bf16[8,768,256]{1,2,0:T(8,128)(2,1)}, u32[]{:S(2)}, u32[]{:S(2)}) async-start(bf16[8,768,256]{1,2,0:T(8,128)(2,1)} %copy.42), calls=%async_computation.1 | async-start | bytes 6291456 | tf_op jit(solution)/shard_map/all_to_all | solution.py:241
  618.2 65.5 %all-to-all-start.3 = ((bf16[8,768,256]{1,2,0:T(8,128)(2,1)}), bf16[8,768,256]{1,2,0:T(8,128)(2,1)}, u32[]{:S(2)}, u32[]{:S(2)}) async-start(bf16[8,768,256]{1,2,0:T(8,128)(2,1)} %copy.44), calls=%async_computation.3 | async-start | bytes 6291456 | tf_op jit(solution)/shard_map/all_to_all | solution.py:241
  646.6 41.7 %copy-start.1 = (bf16[768,2048]{1,0:T(8,128)(2,1)S(1)}, bf16[768,2048]{1,0:T(8,128)(2,1)}, u32[]{:S(2)}) copy-start(bf16[768,2048]{1,0:T(8,128)(2,1)} %param.8) | copy-start | bytes 9437188
  646.6 41.7 %copy-start.6 = (f32[2048]{0:T(1024)S(1)}, f32[2048]{0:T(1024)}, u32[]{:S(2)}) copy-start(f32[2048]{0:T(1024)} %copy-done.5) | copy-start | bytes 24580
  646.6 41.7 %copy-start.8 = (f32[768]{0:T(1024)S(1)}, f32[768]{0:T(1024)}, u32[]{:S(2)}) copy-start(f32[768]{0:T(1024)} %copy-done.7) | copy-start | bytes 9220
  646.6 41.7 %copy-start.12 = (f32[768]{0:T(1024)S(1)}, f32[768]{0:T(1024)}, u32[]{:S(2)}) copy-start(f32[768]{0:T(1024)} %copy-done.11) | copy-start | bytes 9220
  683.6 57.7 %all-to-all-start = ((bf16[8,768,256]{1,2,0:T(8,128)(2,1)}), bf16[8,768,256]{1,2,0:T(8,128)(2,1)}, u32[]{:S(2)}, u32[]{:S(2)}) async-start(bf16[8,768,256]{1,2,0:T(8,128)(2,1)} %copy.38), calls=%async_computation | async-start | bytes 6291456 | tf_op jit(solution)/shard_map/all_to_all | solution.py:236
  688.3 46.9 %copy-start.10 = (f32[768]{0:T(1024)S(1)}, f32[768]{0:T(1024)}, u32[]{:S(2)}) copy-start(f32[768]{0:T(1024)} %copy-done.9) | copy-start | bytes 9220
Sparse Core Ops, SparseCore 0:
  17.3 119.8 all-gather.7
  138.8 117.5 all-gather.9
  292.6 46.2 all-gather.17
  466.0 61.9 all-gather.11
  529.4 85.2 all-gather.15
  616.7 85.5 all-gather.13

commit v2 on v1

v2 whole, which is shorter than its diff:
```python
import math
import jax
import jax.numpy as jnp
from jax import lax
from jax.experimental import pallas as pl
from jax.experimental.pallas import tpu as pltpu
from jax.sharding import PartitionSpec as P

HEAD_DIM = 128
LN_EPS = 1e-5
ROPE_BASE = 10000.0
SCALE = HEAD_DIM ** -0.5
EXP2_SCALE = SCALE * math.log2(math.e)
BLOCK = 512
SUB = 256
VMEM_LIMIT = 56 * 1024 * 1024
LAST = (((1,), (1,)), ((), ()))
PLAIN = (((1,), (0,)), ((), ()))


def norm_f32(hid_f32, weight_f32):
    mean_val = jnp.mean(hid_f32, axis=-1, keepdims=True)
    centered = hid_f32 - mean_val
    var_val = jnp.mean(centered * centered, axis=-1, keepdims=True)
    return centered * lax.rsqrt(var_val + LN_EPS) * weight_f32


def ln_kernel(x_ref, w_ref, h_ref):
    h_ref[...] = norm_f32(x_ref[...].astype(jnp.float32), w_ref[...]).astype(jnp.bfloat16)


def layer_norm(x, ln_weight):
    rows, width = x.shape
    tile = math.gcd(rows, 128)
    spec = pl.BlockSpec((tile, width), lambda i: (i, 0))
    return pl.pallas_call(
        ln_kernel, grid=(rows // tile,),
        in_specs=[spec, pl.BlockSpec((1, width), lambda i: (0, 0))], out_specs=spec,
        out_shape=jax.ShapeDtypeStruct(x.shape, jnp.bfloat16),
        compiler_params=pltpu.CompilerParams(vmem_limit_bytes=VMEM_LIMIT),
        cost_estimate=pl.CostEstimate(flops=10 * rows * width, bytes_accessed=4 * rows * width, transcendentals=0),
        name="layer_norm",
    )(x, ln_weight)


def rope_tables(positions):
    inv_freq = ROPE_BASE ** (-jnp.arange(0, HEAD_DIM, 2, dtype=jnp.float32) / HEAD_DIM)
    angles = positions.astype(jnp.float32)[:, None] * inv_freq[None, :]
    cos_t, sin_t = jnp.cos(angles), jnp.sin(angles)
    cos_full = jnp.stack([cos_t, cos_t], axis=-1).reshape(-1, HEAD_DIM)
    sin_full = jnp.stack([-sin_t, sin_t], axis=-1).reshape(-1, HEAD_DIM)
    return cos_full, sin_full


def swap_pairs(x):
    lane = lax.broadcasted_iota(jnp.int32, x.shape, 1)
    up = pltpu.roll(x, HEAD_DIM - 1, 1)
    down = pltpu.roll(x, 1, 1)
    return jnp.where(lane % 2 == 0, up, down)


def dot_f32(a, b, dims):
    return lax.dot_general(a, b, dims, preferred_element_type=jnp.float32)


def proj_kernel(h_ref, wq_ref, wk_ref, wv_ref, cos_ref, sin_ref, q_ref, k_ref, v_ref, kt_ref, vt_ref):
    h = h_ref[...]
    cos_t, sin_t = cos_ref[...], sin_ref[...]
    q = dot_f32(h, wq_ref[...], PLAIN)
    k = dot_f32(h, wk_ref[...], PLAIN)
    v = dot_f32(h, wv_ref[...], PLAIN)
    for n in range(q.shape[1] // HEAD_DIM):
        cols = slice(n * HEAD_DIM, (n + 1) * HEAD_DIM)
        qn, kn, vn = q[:, cols], k[:, cols], v[:, cols]
        q_ref[:, cols] = (qn * cos_t + swap_pairs(qn) * sin_t).astype(jnp.bfloat16)
        kn = kn * cos_t + swap_pairs(kn) * sin_t
        k_ref[:, cols] = kn.astype(jnp.bfloat16)
        v_ref[:, cols] = vn.astype(jnp.bfloat16)
        kt_ref[cols, :] = kn.T.astype(jnp.bfloat16)
        vt_ref[cols, :] = vn.T.astype(jnp.bfloat16)


def project(h_all, w_q, w_k, w_v, cos_full, sin_full):
    rows, depth = h_all.shape
    cols = w_q.shape[1]
    tile = BLOCK
    row_spec = lambda width: pl.BlockSpec((tile, width), lambda i: (i, 0))
    full = pl.BlockSpec((depth, cols), lambda i: (0, 0))
    col_spec = pl.BlockSpec((cols, tile), lambda i: (0, i))
    out = jax.ShapeDtypeStruct((rows, cols), jnp.bfloat16)
    out_t = jax.ShapeDtypeStruct((cols, rows), jnp.bfloat16)
    return pl.pallas_call(
        proj_kernel, grid=(rows // tile,),
        in_specs=[row_spec(depth), full, full, full, row_spec(HEAD_DIM), row_spec(HEAD_DIM)],
        out_specs=[row_spec(cols)] * 3 + [col_spec] * 2,
        out_shape=[out] * 3 + [out_t] * 2,
        compiler_params=pltpu.CompilerParams(vmem_limit_bytes=VMEM_LIMIT),
        cost_estimate=pl.CostEstimate(flops=6 * rows * depth * cols, bytes_accessed=2 * rows * (depth + 5 * cols), transcendentals=0),
        name="project",
    )(h_all, w_q, w_k, w_v, cos_full, sin_full)


def causal(st, row0, col0):
    keys = lax.broadcasted_iota(jnp.int32, st.shape, 0) + row0
    qs = lax.broadcasted_iota(jnp.int32, st.shape, 1) + col0
    return jnp.where(keys <= qs, st, -jnp.inf)


def fwd_kernel(q_ref, k_ref, vt_ref, o_ref, ot_ref, lse_ref, acc_ref, m_ref, l_ref):
    i = pl.program_id(1)
    rows = q_ref.shape[0]
    acc_ref[...] = jnp.zeros_like(acc_ref)
    m_ref[...] = jnp.full_like(m_ref, -jnp.inf)
    l_ref[...] = jnp.zeros_like(l_ref)

    def step(j, diagonal):
        start = pl.multiple_of(j * rows, rows)

        def scores(a):
            keys = a + SUB if diagonal else rows
            st = dot_f32(k_ref[pl.ds(start, keys), :], q_ref[a:a + SUB, :], LAST)
            return causal(st, 0, a) if diagonal else st

        def update(a, st):
            cols = slice(a, a + SUB)
            m = m_ref[:, cols]
            m_new = jnp.maximum(m, jnp.max(st, axis=0, keepdims=True))
            p = jnp.exp2((st - m_new) * EXP2_SCALE)
            alpha = jnp.exp2((m - m_new) * EXP2_SCALE)
            m_ref[:, cols] = m_new
            l_ref[:, cols] = l_ref[:, cols] * alpha + jnp.sum(p, axis=0, keepdims=True)
            pv = dot_f32(vt_ref[:, pl.ds(start, st.shape[0])], p.astype(jnp.bfloat16), PLAIN)
            acc_ref[:, cols] = acc_ref[:, cols] * alpha + pv

        st = scores(0)
        for a in range(0, rows, SUB):
            ahead = scores(a + SUB) if a + SUB < rows else None
            update(a, st)
            st = ahead

    lax.fori_loop(0, i, lambda j, c: (step(j, False), c)[1], 0)
    step(i, True)
    ot = acc_ref[...] / l_ref[...]
    ot_ref[...] = ot
    o_ref[...] = ot.T.astype(jnp.bfloat16)
    lse_ref[0] = m_ref[...] * EXP2_SCALE + jnp.log2(l_ref[...])


def attn_forward(q, k, vt, block):
    rows, cols = q.shape
    heads = cols // HEAD_DIM
    flops = 2 * 2 * rows * rows * cols // 2
    return pl.pallas_call(
        fwd_kernel, grid=(heads, rows // block),
        in_specs=[pl.BlockSpec((block, HEAD_DIM), lambda h, i: (i, h)),
                  pl.BlockSpec((rows, HEAD_DIM), lambda h, i: (0, h)),
                  pl.BlockSpec((HEAD_DIM, rows), lambda h, i: (h, 0))],
        out_specs=[pl.BlockSpec((block, HEAD_DIM), lambda h, i: (i, h)),
                   pl.BlockSpec((HEAD_DIM, block), lambda h, i: (h, i)),
                   pl.BlockSpec((1, 1, block), lambda h, i: (h, 0, i))],
        out_shape=[jax.ShapeDtypeStruct((rows, cols), jnp.bfloat16),
                   jax.ShapeDtypeStruct((cols, rows), jnp.float32),
                   jax.ShapeDtypeStruct((heads, 1, rows), jnp.float32)],
        scratch_shapes=[pltpu.VMEM((HEAD_DIM, block), jnp.float32),
                        pltpu.VMEM((1, block), jnp.float32),
                        pltpu.VMEM((1, block), jnp.float32)],
        compiler_params=pltpu.CompilerParams(vmem_limit_bytes=VMEM_LIMIT),
        cost_estimate=pl.CostEstimate(flops=2 * flops, bytes_accessed=10 * rows * cols, transcendentals=0),
        name="attn_fwd",
    )(q, k, vt)


def unrope(x, cos_t, sin_t):
    x = x.astype(jnp.bfloat16).astype(jnp.float32)
    return (x * cos_t - swap_pairs(x) * sin_t).astype(jnp.bfloat16)


def bwd_kernel(q_ref, do_ref, ot_ref, lse_ref, k_ref, v_ref, kt_ref, cos_ref, sin_ref,
               g_ref, dk_acc, dv_acc, dqt_acc):
    i = pl.program_id(0)
    rows = q_ref.shape[0]

    @pl.when(i == 0)
    def _():
        dk_acc[...] = jnp.zeros_like(dk_acc)
        dv_acc[...] = jnp.zeros_like(dv_acc)

    lse = lse_ref[0]
    row_dot = jnp.sum(do_ref[...].astype(jnp.float32).T * ot_ref[...], axis=0, keepdims=True)
    dqt_acc[...] = jnp.zeros_like(dqt_acc)

    def step(j, diagonal):
        start = pl.multiple_of(j * rows, rows)

        def scores(b):
            first = b if diagonal else 0
            keys = pl.ds(start + b, SUB)
            st = dot_f32(k_ref[keys, :], q_ref[first:, :], LAST)
            dpt = dot_f32(v_ref[keys, :], do_ref[first:, :], LAST)
            return st, dpt

        def update(b, st, dpt):
            first = b if diagonal else 0
            keys = pl.ds(start + b, SUB)
            if diagonal:
                st = causal(st, b, first)
            p = jnp.exp2(st * EXP2_SCALE - lse[:, first:])
            ds = (p * (dpt - row_dot[:, first:]) * SCALE).astype(jnp.bfloat16)
            dv_acc[keys, :] += dot_f32(p.astype(jnp.bfloat16), do_ref[first:, :], PLAIN)
            dk_acc[keys, :] += dot_f32(ds, q_ref[first:, :], PLAIN)
            dqt_acc[:, first:] += dot_f32(kt_ref[:, keys], ds, PLAIN)

        now = scores(0)
        for b in range(0, rows, SUB):
            ahead = scores(b + SUB) if b + SUB < rows else None
            update(b, *now)
            now = ahead

    lax.fori_loop(0, i, lambda j, c: (step(j, False), c)[1], 0)
    step(i, True)
    tile = pl.ds(pl.multiple_of(i * rows, rows), rows)
    g_ref[tile, :HEAD_DIM] = unrope(dqt_acc[...].T, cos_ref[tile, :], sin_ref[tile, :])

    @pl.when(i == pl.num_programs(0) - 1)
    def _():
        def finish(j, c):
            part = pl.ds(pl.multiple_of(j * rows, rows), rows)
            g_ref[part, HEAD_DIM:2 * HEAD_DIM] = unrope(dk_acc[part, :], cos_ref[part, :], sin_ref[part, :])
            g_ref[part, 2 * HEAD_DIM:] = dv_acc[part, :].astype(jnp.bfloat16)
            return c

        lax.fori_loop(0, dk_acc.shape[0] // rows, finish, 0)


def attn_backward(q, do, ot, lse, k, v, kt, cos_full, sin_full, block, head):
    rows = q.shape[0]
    flops = 2 * rows * rows * HEAD_DIM // 2
    q_spec = pl.BlockSpec((block, HEAD_DIM), lambda i: (i, head))
    all_spec = pl.BlockSpec((rows, HEAD_DIM), lambda i: (0, head))
    table = pl.BlockSpec((rows, HEAD_DIM), lambda i: (0, 0))
    return pl.pallas_call(
        bwd_kernel, grid=(rows // block,),
        in_specs=[q_spec, q_spec,
                  pl.BlockSpec((HEAD_DIM, block), lambda i: (head, i)),
                  pl.BlockSpec((1, 1, block), lambda i: (head, 0, i)),
                  all_spec, all_spec,
                  pl.BlockSpec((HEAD_DIM, rows), lambda i: (head, 0)),
                  table, table],
        out_specs=pl.BlockSpec((rows, 3 * HEAD_DIM), lambda i: (0, 0)),
        out_shape=jax.ShapeDtypeStruct((rows, 3 * HEAD_DIM), jnp.bfloat16),
        scratch_shapes=[pltpu.VMEM((rows, HEAD_DIM), jnp.float32),
                        pltpu.VMEM((rows, HEAD_DIM), jnp.float32),
                        pltpu.VMEM((HEAD_DIM, block), jnp.float32)],
        compiler_params=pltpu.CompilerParams(vmem_limit_bytes=VMEM_LIMIT),
        cost_estimate=pl.CostEstimate(flops=2 * 5 * flops, bytes_accessed=20 * rows * HEAD_DIM, transcendentals=0),
        name="attn_bwd",
    )(q, do, ot, lse, k, v, kt, cos_full, sin_full)


def out_kernel(o_ref, w_ref, slab_ref, a_ref, dwo_ref, acc_ref):
    d = pl.program_id(0)
    dwo_ref[...] = slab_ref[...]

    @pl.when(d == 0)
    def _():
        acc_ref[...] = jnp.zeros_like(acc_ref)

    acc_ref[...] += dot_f32(o_ref[0], w_ref[...], PLAIN)

    @pl.when(d == pl.num_programs(0) - 1)
    def _():
        a_ref[...] = acc_ref[...].astype(jnp.bfloat16)


def out_project(o_chunks, w_o, dwo_slab):
    n, rows, cols = o_chunks.shape
    width = w_o.shape[1]
    return pl.pallas_call(
        out_kernel, grid=(n,),
        in_specs=[pl.BlockSpec((1, rows, cols), lambda d: (d, 0, 0)),
                  pl.BlockSpec((cols, width), lambda d: (d, 0)),
                  pl.BlockSpec((cols, width), lambda d: (d, 0))],
        out_specs=[pl.BlockSpec((rows, width), lambda d: (0, 0)),
                   pl.BlockSpec((cols, width), lambda d: (d, 0))],
        out_shape=[jax.ShapeDtypeStruct((rows, width), jnp.bfloat16),
                   jax.ShapeDtypeStruct(w_o.shape, jnp.bfloat16)],
        scratch_shapes=[pltpu.VMEM((rows, width), jnp.float32)],
        compiler_params=pltpu.CompilerParams(vmem_limit_bytes=VMEM_LIMIT),
        cost_estimate=pl.CostEstimate(flops=2 * n * rows * cols * width, bytes_accessed=2 * n * cols * (rows + width), transcendentals=0),
        name="out_project",
    )(o_chunks, w_o, dwo_slab)


def tail_kernel(ga_ref, gb_ref, wq_ref, wk_ref, wv_ref, x_ref, lnw_ref, dx_ref, dlnw_ref, acc_ref):
    d = pl.program_id(0)

    @pl.when(d == 0)
    def _():
        acc_ref[...] = jnp.zeros_like(acc_ref)

    for part, w_ref in enumerate((wq_ref, wk_ref, wv_ref)):
        cols = slice(part * HEAD_DIM, (part + 1) * HEAD_DIM)
        both = jnp.concatenate([ga_ref[0, :, cols], gb_ref[0, :, cols]], axis=1)
        acc_ref[...] += dot_f32(both, w_ref[...], LAST)

    @pl.when(d == pl.num_programs(0) - 1)
    def _():
        dlnw_ref[...] = jnp.zeros_like(dlnw_ref)
        lnw = lnw_ref[...]
        step = 64

        def rows_step(t, c):
            rows = pl.ds(pl.multiple_of(t * step, step), step)
            x = x_ref[rows, :].astype(jnp.float32)
            dh = acc_ref[rows, :]
            centered = x - jnp.mean(x, axis=-1, keepdims=True)
            rstd = lax.rsqrt(jnp.mean(centered * centered, axis=-1, keepdims=True) + LN_EPS)
            xhat = centered * rstd
            dlnw_ref[...] += jnp.sum(dh * xhat, axis=0, keepdims=True)
            dxhat = dh * lnw
            dx = rstd * (dxhat - jnp.mean(dxhat, axis=-1, keepdims=True) - xhat * jnp.mean(dxhat * xhat, axis=-1, keepdims=True))
            dx_ref[rows, :] = dx.astype(jnp.bfloat16)
            return c

        lax.fori_loop(0, x_ref.shape[0] // step, rows_step, 0)


def tail(ga, gb, w_q, w_k, w_v, hidden, ln_weight):
    n, rows, cols = ga.shape
    width = hidden.shape[1]
    g_spec = pl.BlockSpec((1, rows, cols), lambda d: (d, 0, 0))
    w_spec = pl.BlockSpec((width, 2 * HEAD_DIM), lambda d: (0, d))
    whole = pl.BlockSpec((rows, width), lambda d: (0, 0))
    row = pl.BlockSpec((1, width), lambda d: (0, 0))
    return pl.pallas_call(
        tail_kernel, grid=(n,),
        in_specs=[g_spec, g_spec, w_spec, w_spec, w_spec, whole, row],
        out_specs=[whole, row],
        out_shape=[jax.ShapeDtypeStruct((rows, width), jnp.bfloat16), jax.ShapeDtypeStruct((1, width), jnp.float32)],
        scratch_shapes=[pltpu.VMEM((rows, width), jnp.float32)],
        compiler_params=pltpu.CompilerParams(vmem_limit_bytes=VMEM_LIMIT),
        cost_estimate=pl.CostEstimate(flops=4 * n * rows * cols * width, bytes_accessed=4 * n * cols * (rows + width), transcendentals=0),
        name="tail",
    )(ga, gb, w_q, w_k, w_v, hidden, ln_weight)


def assemble_kernel(slab_ref, *refs):
    for part, out in enumerate(refs[-3:]):
        out[...] = slab_ref[0, :, part * HEAD_DIM:(part + 1) * HEAD_DIM]


def assemble(slab, head, heads, into=()):
    n, rows, cols = slab.shape
    out_spec = pl.BlockSpec((rows, HEAD_DIM), lambda d: (0, heads * d + head))
    out = jax.ShapeDtypeStruct((rows, n * heads * HEAD_DIM), jnp.bfloat16)
    return pl.pallas_call(
        assemble_kernel, grid=(n,),
        in_specs=[pl.BlockSpec((1, rows, cols), lambda d: (d, 0, 0))] + [pl.BlockSpec(memory_space=pl.ANY)] * len(into),
        out_specs=[out_spec] * 3, out_shape=[out] * 3,
        input_output_aliases={1 + i: i for i in range(len(into))},
        compiler_params=pltpu.CompilerParams(vmem_limit_bytes=VMEM_LIMIT),
        cost_estimate=pl.CostEstimate(flops=rows * n * cols * 64, bytes_accessed=4 * n * rows * cols, transcendentals=0),
        name="assemble",
    )(slab, *into)


def solution(mesh):
    sp_size = mesh.shape['sp']
    row_spec = P(('dp', 'sp'), None)
    pos_spec = P(('dp', 'sp'))
    full_spec = P(None, None)
    grad_spec = P('dp', None)

    def layer(hidden, positions, d_attn, ln_weight, w_q, w_k, w_v, w_o):
        me = lax.axis_index('sp')
        block = hidden.shape[0]
        cols = w_q.shape[1] // sp_size
        lnw32 = ln_weight.astype(jnp.float32)
        normed = layer_norm(hidden, lnw32[None])
        pos_all = lax.all_gather(positions, 'sp', tiled=True)
        h_all = lax.all_gather(normed, 'sp', tiled=True)
        g_all = lax.all_gather(d_attn, 'sp', tiled=True)
        cos_full, sin_full = rope_tables(pos_all)
        mine = lambda w, axis: lax.dynamic_slice_in_dim(w, me * cols, cols, axis)
        wq_my, wk_my, wv_my, wo_my = mine(w_q, 1), mine(w_k, 1), mine(w_v, 1), mine(w_o, 0)
        q, k, v, kt, vt = project(h_all, wq_my, wk_my, wv_my, cos_full, sin_full)

        def exchange(x):
            return lax.all_to_all(x.reshape(sp_size, block, x.shape[1]), 'sp', 0, 0)

        o, ot, lse = attn_forward(q, k, vt, block)
        o_chunks = exchange(o)
        d_o = jnp.einsum('td,ed->te', g_all, wo_my, preferred_element_type=jnp.float32).astype(jnp.bfloat16)

        def back(q, head):
            return attn_backward(q, d_o, ot, lse, k, v, kt, cos_full, sin_full, block, head)

        def wgrad(x):
            return jnp.einsum('td,te->de', h_all, x, preferred_element_type=jnp.float32).astype(jnp.bfloat16)

        dwo_my = jnp.einsum('te,td->ed', o, g_all, preferred_element_type=jnp.float32).astype(jnp.bfloat16)
        q_0, dwo_my = lax.optimization_barrier((q, dwo_my))
        dwo_slab = lax.all_gather(dwo_my, 'sp', tiled=True)
        g_a = back(q_0, 0)
        sent_a, o_chunks = lax.optimization_barrier((g_a, o_chunks))
        ga_tok = exchange(sent_a)
        q_1, part_a = lax.optimization_barrier((q, wgrad(g_a)))
        slab_a = lax.all_gather(part_a, 'sp')
        g_b = back(q_1, 1)
        sent_b, ga_tok = lax.optimization_barrier((g_b, ga_tok))
        gb_tok = exchange(sent_b)
        slab_b = lax.all_gather(wgrad(g_b), 'sp')
        attn_out, dw_o = out_project(o_chunks, w_o, dwo_slab)
        d_hid, d_lnw = tail(ga_tok, gb_tok, w_q, w_k, w_v, hidden, lnw32[None])
        d_lnw = lax.psum(d_lnw[0], 'sp').astype(jnp.bfloat16)
        half = assemble(slab_a, 0, 2)
        half, d_hid, attn_out, slab_b = lax.optimization_barrier((half, d_hid, attn_out, slab_b))
        dw_q, dw_k, dw_v = assemble(slab_b, 1, 2, half)
        return attn_out, d_hid, d_lnw, dw_q, dw_k, dw_v, dw_o

    return jax.shard_map(layer, mesh=mesh,
                         in_specs=(row_spec, pos_spec, row_spec, P(None), full_spec, full_spec, full_spec, full_spec),
                         out_specs=(row_spec, row_spec, P('dp'), grad_spec, grad_spec, grad_spec, grad_spec),
                         check_vma=False)
```

time: 798 us -> 759 us (0.951)
  blocking collectives: 54.5 us -> 236 us
  waiting for transfers between devices: 199 us -> 66 us
  matrix products: 120 us -> 69.3 us
  local copies, waits for them, and re-layouts: 76.5 us -> 26.1 us
  Pallas kernels: 288 us -> 329 us
  starting transfers between devices: 19.8 us -> 0.32 us
  other arithmetic: 21.9 us -> 8.99 us
    all_to_all x0 -> x3, blocking collectives: none -> 202 us  [exchange(): return lax.all_to_all(x.reshape(sp_size, block, x.shape[1]), 'sp', 0, 0)]
    all_to_all x4 -> x0, waiting for transfers between devices: 137 us -> none  [the longest x3 137 us: local_step(): to_tok = lambda x: lax.all_to_all(x, 'sp', 0, 1, tiled=True)]
    dot_general x9 -> x4, matrix products: 120 us -> 69.3 us  [the longest x2 40.8 us: wgrad(): jnp.einsum('td,te->de', h_all, x, preferred_element_type=jnp.float32)]
    pallas_call x2 -> x8, Pallas kernels: 258 us -> 298 us  [the longest x2 132 us: attn_backward(): pl.pallas_call(bwd_kernel, grid=(rows // block,), in_specs=[q_spec, q_spe...]
    unnamed x35 -> x11, local copies, waits for them, and re-layouts: 35.6 us -> 0.03 us
    all_to_all x4 -> x0, starting transfers between devices: 19.4 us -> none  [the longest x3 14.8 us: local_step(): to_tok = lambda x: lax.all_to_all(x, 'sp', 0, 1, tiled=True)]
    psum x1, blocking collectives: 29.8 us -> 14.1 us  [layer(): d_lnw = lax.psum(d_lnw[0], 'sp').astype(jnp.bfloat16)]
    all_to_all x4 -> x0, local copies, waits for them, and re-layouts: 15 us -> none  [the longest x3 12.2 us: local_step(): to_tok = lambda x: lax.all_to_all(x, 'sp', 0, 1, tiled=True)]
  transfers between devices with their start and end apart: 10 -> 5, of which waited for: 4 -> 2; matrix products, arithmetic and copies ran while one was open for 20% -> 12% of each run, Pallas kernels for 36% -> 41%
where the time goes in v2:
time: 759 us; the launch traced here: 750 us
  Pallas kernels  329 us (43%)
  blocking collectives  236 us (31%)
  matrix products  69.3 us (9%)
  waiting for transfers between devices  66 us (9%)
  local copies, waits for them, and re-layouts  26.1 us (3%)
  between operations  14.1 us (2%)
  other arithmetic  8.99 us (1%)
    all_to_all x3, blocking collectives, exchange(): return lax.all_to_all(x.reshape(sp_size, block, x.shape[1]), 'sp', 0, 0)  202 us
    pallas_call x2, Pallas kernels, attn_backward(): pl.pallas_call(bwd_kernel, grid=(rows // block,), in_specs=[q_spec, q_spe...  132 us
    pallas_call x1, Pallas kernels, attn_forward(): pl.pallas_call(fwd_kernel, grid=(heads, rows // block), in_specs=[pl.Bloc...  87.1 us
    all_gather x1, waiting for transfers between devices, layer(): h_all = lax.all_gather(normed, 'sp', tiled=True)  64.2 us
    dot_general x2, matrix products, wgrad(): jnp.einsum('td,te->de', h_all, x, preferred_element_type=jnp.float32)  40.8 us
    pallas_call x1, Pallas kernels, tail(): pl.pallas_call(tail_kernel, grid=(n,), in_specs=[g_spec, g_spec, w_spec,...  32.9 us
    pallas_call x1, Pallas kernels, project(): pl.pallas_call(proj_kernel, grid=(rows // tile,), in_specs=[row_spec(dept...  30.8 us
    pallas_call x2, Pallas kernels, assemble(): pl.pallas_call(assemble_kernel, grid=(n,), in_specs=[pl.BlockSpec((1, row...  23.9 us
  transfers between devices with their start and end apart: 5, of which 2 were waited for; matrix products, arithmetic and copies ran while one was open for 12% of the time, Pallas kernels for 41%

profile of v2, /device:TPU:112, one launch (start us, length us, event | category | flops | bytes accessed | tf_op | source)
XLA Modules:
  0.0 749.8 jit_solution(17326458876673305667)
XLA Ops:
  7.2 0.1 all-gather.9.cloned.1.call-start
  7.2 1.3 broadcast_in_dim.10
  8.5 6.1 layer_norm.1
  14.6 0.0 copy-start.2
  14.6 0.1 all-gather.9.cloned.1.call-update
  14.7 0.1 all-gather.11.cloned.1.call-start
  14.8 0.7 all-gather.11.cloned.1.call-update
  15.5 0.1 all-gather.13.cloned.1.call-start
  15.6 0.0 copy-done.2
  15.6 20.2 %all-gather.2 = s32[8,1,768]{2,1,0:T(1,128)S(1)} all-gather(s32[1,1,768]{2,1,0:T(1,128)S(1)} %reshape.175), channel_id=1, replica_groups=mesh['dp'=2,'sp'=8] {'sp'}, dimensions={0}, use_global_device_ids=true | all-gather | bytes 27648 | tf_op jit(solution)/shard_map/all_gather | solution.py:380
  35.9 5.5 fusion.2
  41.4 2.1 pad_maximum_fusion
  43.6 2.4 copy.33
  46.0 3.5 reshape.167
  49.5 3.6 copy.35.cos_ref
  53.1 4.3 copy.34
  57.4 3.3 reshape.168
  60.7 3.6 copy.36.sin_ref
  64.3 2.3 constant_dynamic-slice_fusion.2.wq_ref
  66.6 3.1 constant_dynamic-slice_fusion
  69.7 64.2 %all-gather.9.cloned.1.call-done.h_ref = bf16[6144,2048]{1,0:T(8,128)(2,1)} async-done(((bf16[768,2048]{1,0:T(8,128)(2,1)}), bf16[6144,2048]{1,0:T(8,128)(2,1)}) %all-gather.9.cloned.1.call-update) | async-done | bytes 25165840 | tf_op jit(solution)/shard_map/all_gather | solution.py:381
  133.9 30.8 %project.1 = (bf16[6144,256]{1,0:T(8,128)(2,1)}, bf16[6144,256]{1,0:T(8,128)(2,1)}, bf16[6144,256]{1,0:T(8,128)(2,1)}, bf16[256,6144]{1,0:T(8,128)(2,1)}, bf16[256,6144]{1,0:T(8,128)(2,1)}) custom-call(bf16[6144,2048]{1,0:T(8,128)(2,1)} %all-gather.9.cloned.1.call-done.h_ref, bf16[2048,256]{1,0:T(8,128)(2,1)} %constant_dynamic-slice_fusion.2.wq_ref, ...), custom_call_target="tpu_custom_call" | custom-call | flops 19327352832 | bytes 40894464 | tf_op jit(solution)/shard_map/project/pallas_call | solution.py:92
  164.6 87.1 %attn_fwd.1 = (bf16[6144,256]{1,0:T(8,128)(2,1)}, f32[256,6144]{1,0:T(8,128)}, f32[2,1,6144]{2,1,0:T(1,128)}) custom-call(bf16[6144,256]{1,0:T(8,128)(2,1)} %get-tuple-element.52.q_ref, bf16[6144,256]{1,0:T(8,128)(2,1)} %get-tuple-element.40.k_ref, bf16[256,6144]{1,0:T(8,128)(2,1)} %get-tuple-element.41.vt_ref), custom_call_target="tpu_custom_call" | custom-call | flops 38654705664 | bytes 15728640 | tf_op jit(solution)/shard_map/attn_fwd/pallas_call | solution.py:153
  251.8 0.8 all-gather.11.cloned.1.call-done
  252.5 13.3 %convolution_convert_fusion.3 = bf16[256,2048]{1,0:T(8,128)(2,1)} fusion(bf16[6144,256]{1,0:T(8,128)(2,1)} %get-tuple-element.42, bf16[6144,2048]{1,0:T(8,128)(2,1)} %all-gather.11.cloned.1.call-done), kind=kOutput, calls=%fused_computation.6 | convolution fusion | flops 6442975232 | bytes 29360128 | tf_op jit(solution)/shard_map/te,td->ed/dot_general | solution.py:401
  265.9 0.1 all-gather.13.cloned.1.call-update
  265.9 0.1 all-gather.15.cloned.1.call-start
  266.0 15.2 %fusion.do_ref = bf16[6144,256]{1,0:T(8,128)(2,1)} fusion(bf16[6144,2048]{1,0:T(8,128)(2,1)} %all-gather.11.cloned.1.call-done, bf16[2048,2048]{1,0:T(8,128)(2,1)} %w_ref.1, s32[]{:T(128)S(6)} %select_n.2), kind=kOutput, calls=%fused_computation.1 | convolution fusion | flops 6444023808 | bytes 29360132 | tf_op jit(solution)/shard_map/td,ed->te/dot_general | solution.py:393
  281.2 65.8 %attn_bwd.2 = bf16[6144,384]{1,0:T(8,128)(2,1)} custom-call(bf16[6144,256]{1,0:T(8,128)(2,1)} %get-tuple-element.52.q_ref, bf16[6144,256]{1,0:T(8,128)(2,1)} %fusion.do_ref, f32[256,6144]{1,0:T(8,128)} %get-tuple-element.44.ot_ref, f32[2,1,6144]{2,1,0:T(1,128)} %get-tuple-element.45.lse_ref, bf16[6144,256]{1,0:T(8,128)(2,1)} %get-tuple-element.40.k_ref, ...), custom_call_target="tpu_custom_call" | custom-call | flops 48318382080 | bytes 15728640 | tf_op jit(solution)/shard_map/attn_bwd/pallas_call | solution.py:241
  347.0 20.5 %convolution_convert_fusion.2 = bf16[2048,384]{1,0:T(8,128)(2,1)} fusion(bf16[6144,2048]{1,0:T(8,128)(2,1)} %all-gather.9.cloned.1.call-done.h_ref, bf16[6144,384]{1,0:T(8,128)(2,1)} %attn_bwd.2), kind=kOutput, calls=%fused_computation.5 | convolution fusion | flops 9664462848 | bytes 31457280 | tf_op jit(solution)/shard_map/td,te->de/dot_general | solution.py:399
  367.6 0.1 all-gather.15.cloned.1.call-update
  367.6 0.1 all-gather.17.cloned.1.call-start
  367.7 65.7 %attn_bwd.3 = bf16[6144,384]{1,0:T(8,128)(2,1)} custom-call(bf16[6144,256]{1,0:T(8,128)(2,1)} %get-tuple-element.52.q_ref, bf16[6144,256]{1,0:T(8,128)(2,1)} %fusion.do_ref, f32[256,6144]{1,0:T(8,128)} %get-tuple-element.44.ot_ref, f32[2,1,6144]{2,1,0:T(1,128)} %get-tuple-element.45.lse_ref, bf16[6144,256]{1,0:T(8,128)(2,1)} %get-tuple-element.40.k_ref, ...), custom_call_target="tpu_custom_call" | custom-call | flops 48318382080 | bytes 15728640 | tf_op jit(solution)/shard_map/attn_bwd/pallas_call | solution.py:241
  433.4 0.0 copy-start
  433.4 20.3 %convolution_convert_fusion.1 = bf16[2048,384]{1,0:T(8,128)(2,1)} fusion(bf16[6144,2048]{1,0:T(8,128)(2,1)} %all-gather.9.cloned.1.call-done.h_ref, bf16[6144,384]{1,0:T(8,128)(2,1)} %attn_bwd.3), kind=kOutput, calls=%fused_computation.4 | convolution fusion | flops 9664462848 | bytes 31457280 | tf_op jit(solution)/shard_map/td,te->de/dot_general | solution.py:399
  453.7 0.1 all-gather.17.cloned.1.call-update
  453.8 0.0 copy-done
  453.8 0.0 copy-start.1
  453.8 73.2 %all_to_all.15.o_ref = bf16[8,768,256]{2,1,0:T(8,128)(2,1)} all-to-all(bf16[8,768,256]{2,1,0:T(8,128)(2,1)S(1)} %bitcast.21), channel_id=1, replica_groups=mesh['dp'=2,'sp'=8] {'sp'}, dimensions={0} | all-to-all | bytes 6291456 | tf_op jit(solution)/shard_map/all_to_all | solution.py:389
  527.0 0.0 slice-start
  527.0 0.0 copy-done.1
  527.0 0.0 slice-start.1
  527.0 69.9 %all_to_all.16.ga_ref = bf16[8,768,384]{2,1,0:T(8,128)(2,1)} all-to-all(bf16[8,768,384]{2,1,0:T(8,128)(2,1)S(1)} %bitcast.24), channel_id=1, replica_groups=mesh['dp'=2,'sp'=8] {'sp'}, dimensions={0} | all-to-all | bytes 9437184 | tf_op jit(solution)/shard_map/all_to_all | solution.py:389
  596.9 0.0 slice-done
  596.9 0.0 slice-done.1
  596.9 58.9 %all_to_all.17.gb_ref = bf16[8,768,384]{2,1,0:T(8,128)(2,1)} all-to-all(bf16[8,768,384]{2,1,0:T(8,128)(2,1)S(1)} %bitcast.27), channel_id=1, replica_groups=mesh['dp'=2,'sp'=8] {'sp'}, dimensions={0} | all-to-all | bytes 9437184 | tf_op jit(solution)/shard_map/all_to_all | solution.py:389
  655.8 32.9 %tail.1 = (bf16[768,2048]{1,0:T(8,128)(2,1)}, f32[1,2048]{1,0:T(1,128)}) custom-call(bf16[8,768,384]{2,1,0:T(8,128)(2,1)} %all_to_all.16.ga_ref, bf16[8,768,384]{2,1,0:T(8,128)(2,1)} %all_to_all.17.gb_ref, bf16[2048,2048]{1,0:T(8,128)(2,1)} %wq_ref.1, bf16[2048,2048]{1,0:T(8,128)(2,1)} %wk_ref.1, bf16[2048,2048]{1,0:T(8,128)(2,1)} %wv_ref.1, ...), custom_call_target="tpu_custom_call" | custom-call | flops 19327352832 | bytes 34603008 | tf_op jit(solution)/shard_map/tail/pallas_call | solution.py:335
  688.6 14.1 %psum.7 = bf16[2048]{0:T(1024)(128)(2,1)} all-reduce(f32[2048]{0:T(1024)} %bitcast.31), channel_id=1, replica_groups=mesh['dp'=2,'sp'=8] {'sp'}, use_global_device_ids=true, to_apply=%region_0.0 | all-reduce | flops 2048 | bytes 12288 | tf_op jit(solution)/shard_map/psum | solution.py:415
  702.8 0.0 all-gather.13.cloned.1.call-done.slab_ref
  702.8 16.4 %out_project.1 = (bf16[768,2048]{1,0:T(8,128)(2,1)}, bf16[2048,2048]{1,0:T(8,128)(2,1)}) custom-call(bf16[8,768,256]{2,1,0:T(8,128)(2,1)} %all_to_all.15.o_ref, bf16[2048,2048]{1,0:T(8,128)(2,1)} %w_ref.1, bf16[2048,2048]{1,0:T(8,128)(2,1)} %all-gather.13.cloned.1.call-done.slab_ref), custom_call_target="tpu_custom_call" | custom-call | flops 6442450944 | bytes 11534336 | tf_op jit(solution)/shard_map/out_project/pallas_call | solution.py:278
  719.2 0.0 all-gather.15.cloned.1.call-done
  719.2 12.0 %assemble.2 = (bf16[2048,2048]{1,0:T(8,128)(2,1)}, bf16[2048,2048]{1,0:T(8,128)(2,1)}, bf16[2048,2048]{1,0:T(8,128)(2,1)}) custom-call(bf16[8,2048,384]{2,1,0:T(8,128)(2,1)} %bitcast.22), custom_call_target="tpu_custom_call" | custom-call | flops 402653184 | bytes 25165824 | tf_op jit(solution)/shard_map/assemble/pallas_call | solution.py:356
  731.1 0.0 all-gather.17.cloned.1.call-done
  731.1 12.0 %assemble.3 = (bf16[2048,2048]{1,0:T(8,128)(2,1)}, bf16[2048,2048]{1,0:T(8,128)(2,1)}, bf16[2048,2048]{1,0:T(8,128)(2,1)}) custom-call(bf16[8,2048,384]{2,1,0:T(8,128)(2,1)} %bitcast.23, bf16[2048,2048]{1,0:T(8,128)(2,1)} %get-tuple-element.64.refs_0_, ...), custom_call_target="tpu_custom_call", output_to_operand_aliasing={{0}: (1, {}), {1}: (2, {}), {2}: (3, {})} | custom-call | flops 402653184 | bytes 25165824 | tf_op jit(solution)/shard_map/assemble/pallas_call | solution.py:356
  (4 shorter events, 0.0 us)
Async XLA Ops:
  7.2 126.7 %all-gather.9.cloned.1.call-start = ((), (), s32[]{:S(2)}) async-start(), calls=%async_computation.3 | async-start | bytes 28311552 | tf_op jit(solution)/shard_map/all_gather | solution.py:381
  14.6 1.0 copy-start.2
  14.7 237.8 %all-gather.11.cloned.1.call-start = ((), (), s32[]{:S(2)}) async-start(), calls=%async_computation.4 | async-start | bytes 28311552 | tf_op jit(solution)/shard_map/all_gather | solution.py:382
  15.5 687.3 %all-gather.13.cloned.1.call-start = ((), (), s32[]{:S(2)}) async-start(), calls=%async_computation.5 | async-start | bytes 9437184 | tf_op jit(solution)/shard_map/all_gather | solution.py:403
  265.9 453.2 %all-gather.15.cloned.1.call-start = ((), (), s32[]{:S(2)}) async-start(), calls=%async_computation.6 | async-start | bytes 14155776 | tf_op jit(solution)/shard_map/all_gather | solution.py:408
  367.6 363.5 %all-gather.17.cloned.1.call-start = ((), (), s32[]{:S(2)}) async-start(), calls=%async_computation.7 | async-start | bytes 14155776 | tf_op jit(solution)/shard_map/all_gather | solution.py:412
  433.4 20.4 %copy-start = (bf16[6144,256]{1,0:T(8,128)(2,1)S(1)}, bf16[6144,256]{1,0:T(8,128)(2,1)}, u32[]{:S(2)}) copy-start(bf16[6144,256]{1,0:T(8,128)(2,1)} %get-tuple-element.42) | copy-start | bytes 9437188
  453.8 73.2 %copy-start.1 = (bf16[6144,384]{1,0:T(8,128)(2,1)S(1)}, bf16[6144,384]{1,0:T(8,128)(2,1)}, u32[]{:S(2)}) copy-start(bf16[6144,384]{1,0:T(8,128)(2,1)} %attn_bwd.2) | copy-start | bytes 14155780
  527.0 69.9 %slice-start = ((s8[4718592]{0:T(1024)(128)(4,1)}), s8[4194304]{0:T(1024)(128)(4,1)S(1)}, s32[]{:S(2)}) async-start(s8[4718592]{0:T(1024)(128)(4,1)} %bitcast.25), calls=%async_computation.8 | async-start | bytes 8388608
  527.0 69.9 %slice-start.1 = ((s8[4718592]{0:T(1024)(128)(4,1)}), s8[524288]{0:T(1024)(128)(4,1)S(1)}, s32[]{:S(2)}) async-start(s8[4718592]{0:T(1024)(128)(4,1)} %bitcast.25), calls=%async_computation.9 | async-start | bytes 1048576
Sparse Core Ops, SparseCore 0:
  14.8 119.0 all-gather.8
  135.4 117.0 all-gather.10
  266.1 46.4 all-gather.12
  367.7 63.3 all-gather.14
  453.9 114.8 all-gather.16

commit v3 on v2

--- a/solution.py
+++ b/solution.py
@@ -257,6 +257,38 @@
     )(q, do, ot, lse, k, v, kt, cos_full, sin_full)
 
 
+def cot_kernel(g_ref, w_ref, ot_ref, do_ref, dw_ref, acc_ref):
+    t = pl.program_id(0)
+
+    @pl.when(t == 0)
+    def _():
+        acc_ref[...] = jnp.zeros_like(acc_ref)
+
+    g = g_ref[...]
+    do_ref[...] = dot_f32(g, w_ref[...], LAST).astype(jnp.bfloat16)
+    acc_ref[...] += dot_f32(ot_ref[...].astype(jnp.bfloat16), g, PLAIN)
+
+    @pl.when(t == pl.num_programs(0) - 1)
+    def _():
+        dw_ref[...] = acc_ref[...].astype(jnp.bfloat16)
+
+
+def cotangents(g_all, wo_my, ot, block):
+    rows, width = g_all.shape
+    cols = wo_my.shape[0]
+    slab = pl.BlockSpec((cols, width), lambda t: (0, 0))
+    return pl.pallas_call(
+        cot_kernel, grid=(rows // block,),
+        in_specs=[pl.BlockSpec((block, width), lambda t: (t, 0)), slab, pl.BlockSpec((cols, block), lambda t: (0, t))],
+        out_specs=[pl.BlockSpec((block, cols), lambda t: (t, 0)), slab],
+        out_shape=[jax.ShapeDtypeStruct((rows, cols), jnp.bfloat16), jax.ShapeDtypeStruct((cols, width), jnp.bfloat16)],
+        scratch_shapes=[pltpu.VMEM((cols, width), jnp.float32)],
+        compiler_params=pltpu.CompilerParams(vmem_limit_bytes=VMEM_LIMIT),
+        cost_estimate=pl.CostEstimate(flops=4 * rows * cols * width, bytes_accessed=2 * rows * (width + 3 * cols), transcendentals=0),
+        name="cotangents",
+    )(g_all, wo_my, ot)
+
+
 def out_kernel(o_ref, w_ref, slab_ref, a_ref, dwo_ref, acc_ref):
     d = pl.program_id(0)
     dwo_ref[...] = slab_ref[...]
@@ -291,17 +323,28 @@
     )(o_chunks, w_o, dwo_slab)
 
 
-def tail_kernel(ga_ref, gb_ref, wq_ref, wk_ref, wv_ref, x_ref, lnw_ref, dx_ref, dlnw_ref, acc_ref):
+def add_head(g_ref, wq_ref, wk_ref, wv_ref, acc_ref):
+    w_qk = jnp.concatenate([wq_ref[...], wk_ref[...]], axis=1)
+    acc_ref[...] += (dot_f32(g_ref[0, :, :2 * HEAD_DIM], w_qk, LAST)
+                     + dot_f32(g_ref[0, :, 2 * HEAD_DIM:], wv_ref[...], LAST))
+
+
+def tail_a_kernel(g_ref, wq_ref, wk_ref, wv_ref, dh_ref):
+    @pl.when(pl.program_id(0) == 0)
+    def _():
+        dh_ref[...] = jnp.zeros_like(dh_ref)
+
+    add_head(g_ref, wq_ref, wk_ref, wv_ref, dh_ref)
+
+
+def tail_b_kernel(g_ref, wq_ref, wk_ref, wv_ref, first_ref, x_ref, lnw_ref, dx_ref, dlnw_ref, acc_ref):
     d = pl.program_id(0)
 
     @pl.when(d == 0)
     def _():
-        acc_ref[...] = jnp.zeros_like(acc_ref)
-
-    for part, w_ref in enumerate((wq_ref, wk_ref, wv_ref)):
-        cols = slice(part * HEAD_DIM, (part + 1) * HEAD_DIM)
-        both = jnp.concatenate([ga_ref[0, :, cols], gb_ref[0, :, cols]], axis=1)
-        acc_ref[...] += dot_f32(both, w_ref[...], LAST)
+        acc_ref[...] = first_ref[...]
+
+    add_head(g_ref, wq_ref, wk_ref, wv_ref, acc_ref)
 
     @pl.when(d == pl.num_programs(0) - 1)
     def _():
@@ -325,23 +368,24 @@
         lax.fori_loop(0, x_ref.shape[0] // step, rows_step, 0)
 
 
-def tail(ga, gb, w_q, w_k, w_v, hidden, ln_weight):
-    n, rows, cols = ga.shape
-    width = hidden.shape[1]
-    g_spec = pl.BlockSpec((1, rows, cols), lambda d: (d, 0, 0))
-    w_spec = pl.BlockSpec((width, 2 * HEAD_DIM), lambda d: (0, d))
+def tail(g_chunks, w_q, w_k, w_v, head, heads, rest=()):
+    n, rows, cols = g_chunks.shape
+    width = w_q.shape[0]
+    w_spec = pl.BlockSpec((width, HEAD_DIM), lambda d: (0, heads * d + head))
     whole = pl.BlockSpec((rows, width), lambda d: (0, 0))
     row = pl.BlockSpec((1, width), lambda d: (0, 0))
-    return pl.pallas_call(
-        tail_kernel, grid=(n,),
-        in_specs=[g_spec, g_spec, w_spec, w_spec, w_spec, whole, row],
-        out_specs=[whole, row],
-        out_shape=[jax.ShapeDtypeStruct((rows, width), jnp.bfloat16), jax.ShapeDtypeStruct((1, width), jnp.float32)],
-        scratch_shapes=[pltpu.VMEM((rows, width), jnp.float32)],
-        compiler_params=pltpu.CompilerParams(vmem_limit_bytes=VMEM_LIMIT),
-        cost_estimate=pl.CostEstimate(flops=4 * n * rows * cols * width, bytes_accessed=4 * n * cols * (rows + width), transcendentals=0),
-        name="tail",
-    )(ga, gb, w_q, w_k, w_v, hidden, ln_weight)
+    dh = jax.ShapeDtypeStruct((rows, width), jnp.float32)
+    last = bool(rest)
+    return pl.pallas_call(
+        tail_b_kernel if last else tail_a_kernel, grid=(n,),
+        in_specs=[pl.BlockSpec((1, rows, cols), lambda d: (d, 0, 0)), w_spec, w_spec, w_spec] + ([whole, whole, row] if last else []),
+        out_specs=[whole, row] if last else whole,
+        out_shape=[jax.ShapeDtypeStruct((rows, width), jnp.bfloat16), jax.ShapeDtypeStruct((1, width), jnp.float32)] if last else dh,
+        scratch_shapes=[pltpu.VMEM((rows, width), jnp.float32)] if last else [],
+        compiler_params=pltpu.CompilerParams(vmem_limit_bytes=VMEM_LIMIT),
+        cost_estimate=pl.CostEstimate(flops=2 * n * rows * cols * width, bytes_accessed=2 * n * cols * (rows + width), transcendentals=0),
+        name="tail_b" if last else "tail_a",
+    )(g_chunks, w_q, w_k, w_v, *rest)
 
 
 def assemble_kernel(slab_ref, *refs):
@@ -390,7 +434,7 @@
 
         o, ot, lse = attn_forward(q, k, vt, block)
         o_chunks = exchange(o)
-        d_o = jnp.einsum('td,ed->te', g_all, wo_my, preferred_element_type=jnp.float32).astype(jnp.bfloat16)
+        d_o, dwo_my = cotangents(g_all, wo_my, ot, block)
 
         def back(q, head):
             return attn_backward(q, d_o, ot, lse, k, v, kt, cos_full, sin_full, block, head)
@@ -398,7 +442,6 @@
         def wgrad(x):
             return jnp.einsum('td,te->de', h_all, x, preferred_element_type=jnp.float32).astype(jnp.bfloat16)
 
-        dwo_my = jnp.einsum('te,td->ed', o, g_all, preferred_element_type=jnp.float32).astype(jnp.bfloat16)
         q_0, dwo_my = lax.optimization_barrier((q, dwo_my))
         dwo_slab = lax.all_gather(dwo_my, 'sp', tiled=True)
         g_a = back(q_0, 0)
@@ -409,12 +452,16 @@
         g_b = back(q_1, 1)
         sent_b, ga_tok = lax.optimization_barrier((g_b, ga_tok))
         gb_tok = exchange(sent_b)
-        slab_b = lax.all_gather(wgrad(g_b), 'sp')
+        part_b = wgrad(g_b)
+        slab_b = lax.all_gather(part_b, 'sp')
+        ga_tok, o_chunks, dwo_slab, part_b = lax.optimization_barrier((ga_tok, o_chunks, dwo_slab, part_b))
+        dh_a = tail(ga_tok, w_q, w_k, w_v, 0, 2)
         attn_out, dw_o = out_project(o_chunks, w_o, dwo_slab)
-        d_hid, d_lnw = tail(ga_tok, gb_tok, w_q, w_k, w_v, hidden, lnw32[None])
+        dh_a, attn_out, dw_o, slab_a = lax.optimization_barrier((dh_a, attn_out, dw_o, slab_a))
+        half = assemble(slab_a, 0, 2)
+        d_hid, d_lnw = tail(gb_tok, w_q, w_k, w_v, 1, 2, (dh_a, hidden, lnw32[None]))
         d_lnw = lax.psum(d_lnw[0], 'sp').astype(jnp.bfloat16)
-        half = assemble(slab_a, 0, 2)
-        half, d_hid, attn_out, slab_b = lax.optimization_barrier((half, d_hid, attn_out, slab_b))
+        half, d_hid, d_lnw, attn_out, slab_b = lax.optimization_barrier((half, d_hid, d_lnw, attn_out, slab_b))
         dw_q, dw_k, dw_v = assemble(slab_b, 1, 2, half)
         return attn_out, d_hid, d_lnw, dw_q, dw_k, dw_v, dw_o
 

time: 759 us -> 729 us (0.960)
  blocking collectives: 236 us -> 178 us
  Pallas kernels: 329 us -> 362 us
  matrix products: 69.3 us -> 40.5 us
  waiting for transfers between devices: 66 us -> 83 us
    all_to_all x3 -> x2, blocking collectives: 202 us -> 144 us  [exchange(): return lax.all_to_all(x.reshape(sp_size, block, x.shape[1]), 'sp', 0, 0)]
    pallas_call x1 -> x3, Pallas kernels: 32.9 us -> 65.9 us  [the longest x2 46.2 us: tail(): pl.pallas_call(tail_b_kernel if last else tail_a_kernel, grid=(n,), in_sp...]
    dot_general x2 -> x0, matrix products: 28.5 us -> none  [the longest x1 15.2 us: layer(): jnp.einsum('td,ed->te', g_all, wo_my, preferred_element_type=jnp.float32)]
    all_to_all x0 -> x1, waiting for transfers between devices: none -> 19.4 us  [exchange(): return lax.all_to_all(x.reshape(sp_size, block, x.shape[1]), 'sp', 0, 0)]
  transfers between devices with their start and end apart: 5 -> 6, of which waited for: 2 -> 3; matrix products, arithmetic and copies ran while one was open for 12% -> 11% of each run, Pallas kernels for 41% -> 45%
where the time goes in v3:
time: 729 us; the launch traced here: 720 us
  Pallas kernels  362 us (50%)
  blocking collectives  178 us (24%)
  waiting for transfers between devices  83 us (11%)
  matrix products  40.5 us (6%)
  local copies, waits for them, and re-layouts  28.4 us (4%)
  between operations  14.1 us (2%)
  other arithmetic  8.99 us (1%)
    all_to_all x2, blocking collectives, exchange(): return lax.all_to_all(x.reshape(sp_size, block, x.shape[1]), 'sp', 0, 0)  144 us
    pallas_call x2, Pallas kernels, attn_backward(): pl.pallas_call(bwd_kernel, grid=(rows // block,), in_specs=[q_spec, q_spe...  132 us
    pallas_call x1, Pallas kernels, attn_forward(): pl.pallas_call(fwd_kernel, grid=(heads, rows // block), in_specs=[pl.Bloc...  87.1 us
    all_gather x1, waiting for transfers between devices, layer(): h_all = lax.all_gather(normed, 'sp', tiled=True)  61.9 us
    pallas_call x2, Pallas kernels, tail(): pl.pallas_call(tail_b_kernel if last else tail_a_kernel, grid=(n,), in_sp...  46.2 us
    dot_general x2, matrix products, wgrad(): jnp.einsum('td,te->de', h_all, x, preferred_element_type=jnp.float32)  40.5 us
    pallas_call x1, Pallas kernels, project(): pl.pallas_call(proj_kernel, grid=(rows // tile,), in_specs=[row_spec(dept...  30.8 us
    pallas_call x2, Pallas kernels, assemble(): pl.pallas_call(assemble_kernel, grid=(n,), in_specs=[pl.BlockSpec((1, row...  23.9 us
  transfers between devices with their start and end apart: 6, of which 3 were waited for; matrix products, arithmetic and copies ran while one was open for 11% of the time, Pallas kernels for 45%

profile of v3, /device:TPU:112, one launch (start us, length us, event | category | flops | bytes accessed | tf_op | source)
XLA Modules:
  0.0 720.1 jit_solution(3537229311727131736)
XLA Ops:
  7.2 0.1 all-gather.9.cloned.1.call-start
  7.2 1.3 broadcast_in_dim.10
  8.5 6.1 layer_norm.1
  14.6 0.0 copy-start.2
  14.6 0.1 all-gather.9.cloned.1.call-update
  14.7 0.1 all-gather.11.cloned.1.call-start
  14.8 0.7 all-gather.11.cloned.1.call-update
  15.5 0.1 all-gather.13.cloned.1.call-start
  15.6 0.0 copy-done.2
  15.6 20.2 %all-gather.2 = s32[8,1,768]{2,1,0:T(1,128)S(1)} all-gather(s32[1,1,768]{2,1,0:T(1,128)S(1)} %reshape.175), channel_id=1, replica_groups=mesh['dp'=2,'sp'=8] {'sp'}, dimensions={0}, use_global_device_ids=true | all-gather | bytes 27648 | tf_op jit(solution)/shard_map/all_gather | solution.py:424
  35.9 5.5 fusion
  41.4 2.1 pad_maximum_fusion
  43.6 2.4 copy.30
  46.0 3.5 reshape.167
  49.5 3.6 copy.32.cos_ref
  53.1 4.3 copy.31
  57.4 3.3 reshape.168
  60.7 3.6 copy.33.sin_ref
  64.3 2.3 constant_dynamic-slice_fusion.w_ref
  66.6 2.3 constant_dynamic-slice_fusion.3.wq_ref
  68.9 3.1 constant_dynamic-slice_fusion.1
  72.0 61.9 %all-gather.9.cloned.1.call-done.h_ref = bf16[6144,2048]{1,0:T(8,128)(2,1)} async-done(((bf16[768,2048]{1,0:T(8,128)(2,1)}), bf16[6144,2048]{1,0:T(8,128)(2,1)}) %all-gather.9.cloned.1.call-update) | async-done | bytes 25165840 | tf_op jit(solution)/shard_map/all_gather | solution.py:425
  133.9 30.8 %project.1 = (bf16[6144,256]{1,0:T(8,128)(2,1)}, bf16[6144,256]{1,0:T(8,128)(2,1)}, bf16[6144,256]{1,0:T(8,128)(2,1)}, bf16[256,6144]{1,0:T(8,128)(2,1)}, bf16[256,6144]{1,0:T(8,128)(2,1)}) custom-call(bf16[6144,2048]{1,0:T(8,128)(2,1)} %all-gather.9.cloned.1.call-done.h_ref, bf16[2048,256]{1,0:T(8,128)(2,1)} %constant_dynamic-slice_fusion.3.wq_ref, ...), custom_call_target="tpu_custom_call" | custom-call | flops 19327352832 | bytes 40894464 | tf_op jit(solution)/shard_map/project/pallas_call | solution.py:92
  164.6 87.1 %attn_fwd.1 = (bf16[6144,256]{1,0:T(8,128)(2,1)}, f32[256,6144]{1,0:T(8,128)}, f32[2,1,6144]{2,1,0:T(1,128)}) custom-call(bf16[6144,256]{1,0:T(8,128)(2,1)} %get-tuple-element.59.q_ref, bf16[6144,256]{1,0:T(8,128)(2,1)} %get-tuple-element.50.k_ref, bf16[256,6144]{1,0:T(8,128)(2,1)} %get-tuple-element.51.vt_ref), custom_call_target="tpu_custom_call" | custom-call | flops 38654705664 | bytes 15728640 | tf_op jit(solution)/shard_map/attn_fwd/pallas_call | solution.py:153
  251.8 0.8 all-gather.11.cloned.1.call-done.g_ref
  252.5 19.7 %cotangents.1 = (bf16[6144,256]{1,0:T(8,128)(2,1)}, bf16[256,2048]{1,0:T(8,128)(2,1)}) custom-call(bf16[6144,2048]{1,0:T(8,128)(2,1)} %all-gather.11.cloned.1.call-done.g_ref, bf16[256,2048]{1,0:T(8,128)(2,1)} %constant_dynamic-slice_fusion.w_ref, f32[256,6144]{1,0:T(8,128)} %get-tuple-element.52.ot_ref), custom_call_target="tpu_custom_call" | custom-call | flops 12884901888 | bytes 34603008 | tf_op jit(solution)/shard_map/cotangents/pallas_call | solution.py:280
  272.2 0.1 all-gather.13.cloned.1.call-update
  272.3 0.1 all-gather.15.cloned.1.call-start
  272.4 65.8 %attn_bwd.2 = bf16[6144,384]{1,0:T(8,128)(2,1)} custom-call(bf16[6144,256]{1,0:T(8,128)(2,1)} %get-tuple-element.59.q_ref, bf16[6144,256]{1,0:T(8,128)(2,1)} %get-tuple-element.55.do_ref, f32[256,6144]{1,0:T(8,128)} %get-tuple-element.52.ot_ref, f32[2,1,6144]{2,1,0:T(1,128)} %get-tuple-element.56.lse_ref, bf16[6144,256]{1,0:T(8,128)(2,1)} %get-tuple-element.50.k_ref, ...), custom_call_target="tpu_custom_call" | custom-call | flops 48318382080 | bytes 15728640 | tf_op jit(solution)/shard_map/attn_bwd/pallas_call | solution.py:241
  338.2 20.2 %convolution_convert_fusion.1 = bf16[2048,384]{1,0:T(8,128)(2,1)} fusion(bf16[6144,2048]{1,0:T(8,128)(2,1)} %all-gather.9.cloned.1.call-done.h_ref, bf16[6144,384]{1,0:T(8,128)(2,1)} %attn_bwd.2), kind=kOutput, calls=%fused_computation.3 | convolution fusion | flops 9664462848 | bytes 31457280 | tf_op jit(solution)/shard_map/td,te->de/dot_general | solution.py:443
  358.4 0.1 all-gather.15.cloned.1.call-update
  358.5 0.1 all-gather.17.cloned.1.call-start
  358.6 66.1 %attn_bwd.3 = bf16[6144,384]{1,0:T(8,128)(2,1)} custom-call(bf16[6144,256]{1,0:T(8,128)(2,1)} %get-tuple-element.59.q_ref, bf16[6144,256]{1,0:T(8,128)(2,1)} %get-tuple-element.55.do_ref, f32[256,6144]{1,0:T(8,128)} %get-tuple-element.52.ot_ref, f32[2,1,6144]{2,1,0:T(1,128)} %get-tuple-element.56.lse_ref, bf16[6144,256]{1,0:T(8,128)(2,1)} %get-tuple-element.50.k_ref, ...), custom_call_target="tpu_custom_call" | custom-call | flops 48318382080 | bytes 15728640 | tf_op jit(solution)/shard_map/attn_bwd/pallas_call | solution.py:241
  424.6 0.0 copy-start.1
  424.6 20.3 %convolution_convert_fusion = bf16[2048,384]{1,0:T(8,128)(2,1)} fusion(bf16[6144,2048]{1,0:T(8,128)(2,1)} %all-gather.9.cloned.1.call-done.h_ref, bf16[6144,384]{1,0:T(8,128)(2,1)} %attn_bwd.3), kind=kOutput, calls=%fused_computation.2 | convolution fusion | flops 9664462848 | bytes 31457280 | tf_op jit(solution)/shard_map/td,te->de/dot_general | solution.py:443
  445.0 0.1 all-gather.17.cloned.1.call-update
  445.0 0.0 copy-done.1
  445.0 0.0 copy-start
  445.0 73.6 %all_to_all.15.o_ref = bf16[8,768,256]{2,1,0:T(8,128)(2,1)} all-to-all(bf16[8,768,256]{2,1,0:T(8,128)(2,1)S(1)} %bitcast.20), channel_id=1, replica_groups=mesh['dp'=2,'sp'=8] {'sp'}, dimensions={0} | all-to-all | bytes 6291456 | tf_op jit(solution)/shard_map/all_to_all | solution.py:433
  518.6 0.0 copy-done
  518.7 70.1 %all_to_all.16.g_ref = bf16[8,768,384]{2,1,0:T(8,128)(2,1)} all-to-all(bf16[8,768,384]{2,1,0:T(8,128)(2,1)S(1)} %bitcast.19), channel_id=1, replica_groups=mesh['dp'=2,'sp'=8] {'sp'}, dimensions={0} | all-to-all | bytes 9437184 | tf_op jit(solution)/shard_map/all_to_all | solution.py:433
  588.8 5.0 all-to-all-start.2
  593.8 0.0 all-gather.13.cloned.1.call-done.slab_ref
  593.8 16.4 %out_project.1 = (bf16[768,2048]{1,0:T(8,128)(2,1)}, bf16[2048,2048]{1,0:T(8,128)(2,1)}) custom-call(bf16[8,768,256]{2,1,0:T(8,128)(2,1)} %all_to_all.15.o_ref, bf16[2048,2048]{1,0:T(8,128)(2,1)} %w_ref.1, bf16[2048,2048]{1,0:T(8,128)(2,1)} %all-gather.13.cloned.1.call-done.slab_ref), custom_call_target="tpu_custom_call" | custom-call | flops 6442450944 | bytes 11534336 | tf_op jit(solution)/shard_map/out_project/pallas_call | solution.py:310
  610.2 19.3 %tail_a.1.first_ref = f32[768,2048]{1,0:T(8,128)} custom-call(bf16[8,768,384]{2,1,0:T(8,128)(2,1)} %all_to_all.16.g_ref, bf16[2048,2048]{1,0:T(8,128)(2,1)} %wq_ref.3, bf16[2048,2048]{1,0:T(8,128)(2,1)} %wk_ref.3, bf16[2048,2048]{1,0:T(8,128)(2,1)} %wv_ref.3), custom_call_target="tpu_custom_call" | custom-call | flops 9663676416 | bytes 17301504 | tf_op jit(solution)/shard_map/tail_a/pallas_call | solution.py:379
  629.5 0.0 all-gather.15.cloned.1.call-done
  629.5 19.4 %all-to-all-done.2.g_ref = bf16[8,768,384]{2,1,0:T(8,128)(2,1)} async-done(((bf16[8,768,384]{2,1,0:T(8,128)(2,1)}), bf16[8,768,384]{2,1,0:T(8,128)(2,1)}, u32[]{:S(2)}, u32[]{:S(2)}) %all-to-all-start.2) | async-done | bytes 4718624 | tf_op jit(solution)/shard_map/all_to_all | solution.py:433
  648.9 26.9 %tail_b.1 = (bf16[768,2048]{1,0:T(8,128)(2,1)}, f32[1,2048]{1,0:T(1,128)}) custom-call(bf16[8,768,384]{2,1,0:T(8,128)(2,1)} %all-to-all-done.2.g_ref, bf16[2048,2048]{1,0:T(8,128)(2,1)} %wq_ref.3, bf16[2048,2048]{1,0:T(8,128)(2,1)} %wk_ref.3, bf16[2048,2048]{1,0:T(8,128)(2,1)} %wv_ref.3, f32[768,2048]{1,0:T(8,128)} %tail_a.1.first_ref, ...), custom_call_target="tpu_custom_call" | custom-call | flops 9663676416 | bytes 17301504 | tf_op jit(solution)/shard_map/tail_b/pallas_call | solution.py:379
  675.9 13.6 %psum.7 = bf16[2048]{0:T(1024)(128)(2,1)} all-reduce(f32[2048]{0:T(1024)} %bitcast.24), channel_id=1, replica_groups=mesh['dp'=2,'sp'=8] {'sp'}, use_global_device_ids=true, to_apply=%region_0.0 | all-reduce | flops 2048 | bytes 12288 | tf_op jit(solution)/shard_map/psum | solution.py:463
  689.4 11.9 %assemble.2 = (bf16[2048,2048]{1,0:T(8,128)(2,1)}, bf16[2048,2048]{1,0:T(8,128)(2,1)}, bf16[2048,2048]{1,0:T(8,128)(2,1)}) custom-call(bf16[8,2048,384]{2,1,0:T(8,128)(2,1)} %bitcast.16), custom_call_target="tpu_custom_call" | custom-call | flops 402653184 | bytes 25165824 | tf_op jit(solution)/shard_map/assemble/pallas_call | solution.py:400
  701.4 0.0 all-gather.17.cloned.1.call-done
  701.4 12.0 %assemble.3 = (bf16[2048,2048]{1,0:T(8,128)(2,1)}, bf16[2048,2048]{1,0:T(8,128)(2,1)}, bf16[2048,2048]{1,0:T(8,128)(2,1)}) custom-call(bf16[8,2048,384]{2,1,0:T(8,128)(2,1)} %bitcast.17, bf16[2048,2048]{1,0:T(8,128)(2,1)} %get-tuple-element.84.refs_0_, ...), custom_call_target="tpu_custom_call", output_to_operand_aliasing={{0}: (1, {}), {1}: (2, {}), {2}: (3, {})} | custom-call | flops 402653184 | bytes 25165824 | tf_op jit(solution)/shard_map/assemble/pallas_call | solution.py:400
  (3 shorter events, 0.0 us)
Async XLA Ops:
  7.2 126.7 %all-gather.9.cloned.1.call-start = ((), (), s32[]{:S(2)}) async-start(), calls=%async_computation.3 | async-start | bytes 28311552 | tf_op jit(solution)/shard_map/all_gather | solution.py:425
  14.6 1.0 copy-start.2
  14.7 237.8 %all-gather.11.cloned.1.call-start = ((), (), s32[]{:S(2)}) async-start(), calls=%async_computation.4 | async-start | bytes 28311552 | tf_op jit(solution)/shard_map/all_gather | solution.py:426
  15.5 578.3 %all-gather.13.cloned.1.call-start = ((), (), s32[]{:S(2)}) async-start(), calls=%async_computation.5 | async-start | bytes 9437184 | tf_op jit(solution)/shard_map/all_gather | solution.py:446
  272.3 357.2 %all-gather.15.cloned.1.call-start = ((), (), s32[]{:S(2)}) async-start(), calls=%async_computation.6 | async-start | bytes 14155776 | tf_op jit(solution)/shard_map/all_gather | solution.py:451
  358.5 342.9 %all-gather.17.cloned.1.call-start = ((), (), s32[]{:S(2)}) async-start(), calls=%async_computation.7 | async-start | bytes 14155776 | tf_op jit(solution)/shard_map/all_gather | solution.py:456
  424.6 20.4 %copy-start.1 = (bf16[6144,256]{1,0:T(8,128)(2,1)S(1)}, bf16[6144,256]{1,0:T(8,128)(2,1)}, u32[]{:S(2)}) copy-start(bf16[6144,256]{1,0:T(8,128)(2,1)} %get-tuple-element.60) | copy-start | bytes 9437188
  445.0 73.6 %copy-start = (bf16[6144,384]{1,0:T(8,128)(2,1)S(1)}, bf16[6144,384]{1,0:T(8,128)(2,1)}, u32[]{:S(2)}) copy-start(bf16[6144,384]{1,0:T(8,128)(2,1)} %attn_bwd.2) | copy-start | bytes 14155780
  588.8 60.2 %all-to-all-start.2 = ((bf16[8,768,384]{2,1,0:T(8,128)(2,1)}), bf16[8,768,384]{2,1,0:T(8,128)(2,1)}, u32[]{:S(2)}, u32[]{:S(2)}) async-start(bf16[8,768,384]{2,1,0:T(8,128)(2,1)} %bitcast.18), calls=%async_computation.2 | async-start | bytes 9437184 | tf_op jit(solution)/shard_map/all_to_all | solution.py:433
Sparse Core Ops, SparseCore 0:
  14.8 119.0 all-gather.8
  135.4 117.0 all-gather.10
  272.4 46.4 all-gather.12
  358.6 64.1 all-gather.14
  445.1 115.8 all-gather.16

commit v4 on v3

--- a/solution.py
+++ b/solution.py
@@ -11,8 +11,8 @@
 ROPE_BASE = 10000.0
 SCALE = HEAD_DIM ** -0.5
 EXP2_SCALE = SCALE * math.log2(math.e)
-BLOCK = 512
 SUB = 256
+CORES = 2
 VMEM_LIMIT = 56 * 1024 * 1024
 LAST = (((1,), (1,)), ((), ()))
 PLAIN = (((1,), (0,)), ((), ()))
@@ -44,12 +44,11 @@
 
 
 def rope_tables(positions):
-    inv_freq = ROPE_BASE ** (-jnp.arange(0, HEAD_DIM, 2, dtype=jnp.float32) / HEAD_DIM)
+    lane = jnp.arange(HEAD_DIM)
+    inv_freq = ROPE_BASE ** (-(lane - lane % 2).astype(jnp.float32) / HEAD_DIM)
     angles = positions.astype(jnp.float32)[:, None] * inv_freq[None, :]
-    cos_t, sin_t = jnp.cos(angles), jnp.sin(angles)
-    cos_full = jnp.stack([cos_t, cos_t], axis=-1).reshape(-1, HEAD_DIM)
-    sin_full = jnp.stack([-sin_t, sin_t], axis=-1).reshape(-1, HEAD_DIM)
-    return cos_full, sin_full
+    sin_t = jnp.sin(angles)
+    return jnp.cos(angles), jnp.where(lane % 2 == 0, -sin_t, sin_t)
 
 
 def swap_pairs(x):
@@ -63,8 +62,9 @@
     return lax.dot_general(a, b, dims, preferred_element_type=jnp.float32)
 
 
-def proj_kernel(h_ref, wq_ref, wk_ref, wv_ref, cos_ref, sin_ref, q_ref, k_ref, v_ref, kt_ref, vt_ref):
-    h = h_ref[...]
+def proj_kernel(core_ref, h_ref, wq_ref, wk_ref, wv_ref, cos_ref, sin_ref, *refs):
+    q_ref, k_ref, v_ref, kt_ref, vt_ref = refs[-5:]
+    h = h_ref[0]
     cos_t, sin_t = cos_ref[...], sin_ref[...]
     q = dot_f32(h, wq_ref[...], PLAIN)
     k = dot_f32(h, wk_ref[...], PLAIN)
@@ -80,24 +80,28 @@
         vt_ref[cols, :] = vn.T.astype(jnp.bfloat16)
 
 
-def project(h_all, w_q, w_k, w_v, cos_full, sin_full):
-    rows, depth = h_all.shape
+def project(h_half, core, w_q, w_k, w_v, cos_full, sin_full, into=()):
+    chips, block, depth = h_half.shape
+    rows = chips * CORES * block
     cols = w_q.shape[1]
-    tile = BLOCK
-    row_spec = lambda width: pl.BlockSpec((tile, width), lambda i: (i, 0))
-    full = pl.BlockSpec((depth, cols), lambda i: (0, 0))
-    col_spec = pl.BlockSpec((cols, tile), lambda i: (0, i))
+    row_spec = lambda width: pl.BlockSpec((block, width), lambda c, core: (CORES * c + core[0], 0))
+    full = pl.BlockSpec((depth, cols), lambda c, core: (0, 0))
+    col_spec = pl.BlockSpec((cols, block), lambda c, core: (0, CORES * c + core[0]))
     out = jax.ShapeDtypeStruct((rows, cols), jnp.bfloat16)
     out_t = jax.ShapeDtypeStruct((cols, rows), jnp.bfloat16)
     return pl.pallas_call(
-        proj_kernel, grid=(rows // tile,),
-        in_specs=[row_spec(depth), full, full, full, row_spec(HEAD_DIM), row_spec(HEAD_DIM)],
-        out_specs=[row_spec(cols)] * 3 + [col_spec] * 2,
+        proj_kernel,
+        grid_spec=pltpu.PrefetchScalarGridSpec(
+            num_scalar_prefetch=1, grid=(chips,),
+            in_specs=[pl.BlockSpec((1, block, depth), lambda c, core: (c, 0, 0)), full, full, full,
+                      row_spec(HEAD_DIM), row_spec(HEAD_DIM)] + [pl.BlockSpec(memory_space=pl.ANY)] * len(into),
+            out_specs=[row_spec(cols)] * 3 + [col_spec] * 2),
         out_shape=[out] * 3 + [out_t] * 2,
-        compiler_params=pltpu.CompilerParams(vmem_limit_bytes=VMEM_LIMIT),
-        cost_estimate=pl.CostEstimate(flops=6 * rows * depth * cols, bytes_accessed=2 * rows * (depth + 5 * cols), transcendentals=0),
+        input_output_aliases={7 + i: i for i in range(len(into))},
+        compiler_params=pltpu.CompilerParams(vmem_limit_bytes=VMEM_LIMIT),
+        cost_estimate=pl.CostEstimate(flops=6 * chips * block * depth * cols, bytes_accessed=2 * chips * block * (depth + 5 * cols), transcendentals=0),
         name="project",
-    )(h_all, w_q, w_k, w_v, cos_full, sin_full)
+    )(core, h_half, w_q, w_k, w_v, cos_full, sin_full, *into)
 
 
 def causal(st, row0, col0):
@@ -422,12 +426,20 @@
         lnw32 = ln_weight.astype(jnp.float32)
         normed = layer_norm(hidden, lnw32[None])
         pos_all = lax.all_gather(positions, 'sp', tiled=True)
-        h_all = lax.all_gather(normed, 'sp', tiled=True)
-        g_all = lax.all_gather(d_attn, 'sp', tiled=True)
+        same_core = [[d for d in range(sp_size) if d % CORES == c] for c in range(CORES)]
+        normed, d_attn = lax.optimization_barrier((normed, d_attn))
+        h_own = lax.all_gather(normed, 'sp', axis_index_groups=same_core)
         cos_full, sin_full = rope_tables(pos_all)
         mine = lambda w, axis: lax.dynamic_slice_in_dim(w, me * cols, cols, axis)
         wq_my, wk_my, wv_my, wo_my = mine(w_q, 1), mine(w_k, 1), mine(w_v, 1), mine(w_o, 0)
-        q, k, v, kt, vt = project(h_all, wq_my, wk_my, wv_my, cos_full, sin_full)
+        h_own, cos_full, sin_full, wq_my, wk_my, wv_my, wo_my = lax.optimization_barrier(
+            (h_own, cos_full, sin_full, wq_my, wk_my, wv_my, wo_my))
+        h_other = lax.ppermute(h_own, 'sp', [(d, d ^ 1) for d in range(sp_size)])
+        g_all = lax.all_gather(d_attn, 'sp', tiled=True)
+        core = (me % CORES).astype(jnp.int32)
+        partner = CORES - 1 - core
+        mine_done = project(h_own, core[None], wq_my, wk_my, wv_my, cos_full, sin_full)
+        q, k, v, kt, vt = project(h_other, partner[None], wq_my, wk_my, wv_my, cos_full, sin_full, mine_done)
 
         def exchange(x):
             return lax.all_to_all(x.reshape(sp_size, block, x.shape[1]), 'sp', 0, 0)
@@ -440,7 +452,9 @@
             return attn_backward(q, d_o, ot, lse, k, v, kt, cos_full, sin_full, block, head)
 
         def wgrad(x):
-            return jnp.einsum('td,te->de', h_all, x, preferred_element_type=jnp.float32).astype(jnp.bfloat16)
+            blocks = x.reshape(sp_size // CORES, CORES, block, x.shape[1])
+            half = lambda h, c: jnp.einsum('ctd,cte->de', h, lax.dynamic_index_in_dim(blocks, c, 1, False), preferred_element_type=jnp.float32)
+            return (half(h_own, core) + half(h_other, partner)).astype(jnp.bfloat16)
 
         q_0, dwo_my = lax.optimization_barrier((q, dwo_my))
         dwo_slab = lax.all_gather(dwo_my, 'sp', tiled=True)
@@ -460,8 +474,9 @@
         dh_a, attn_out, dw_o, slab_a = lax.optimization_barrier((dh_a, attn_out, dw_o, slab_a))
         half = assemble(slab_a, 0, 2)
         d_hid, d_lnw = tail(gb_tok, w_q, w_k, w_v, 1, 2, (dh_a, hidden, lnw32[None]))
-        d_lnw = lax.psum(d_lnw[0], 'sp').astype(jnp.bfloat16)
-        half, d_hid, d_lnw, attn_out, slab_b = lax.optimization_barrier((half, d_hid, d_lnw, attn_out, slab_b))
+        parts = lax.all_to_all(jnp.broadcast_to(d_lnw[None], (sp_size,) + d_lnw.shape), 'sp', 0, 0)
+        d_lnw = jnp.sum(parts, axis=(0, 1)).astype(jnp.bfloat16)
+        half, d_hid, attn_out, slab_b = lax.optimization_barrier((half, d_hid, attn_out, slab_b))
         dw_q, dw_k, dw_v = assemble(slab_b, 1, 2, half)
         return attn_out, d_hid, d_lnw, dw_q, dw_k, dw_v, dw_o
 

time: 729 us -> 733 us (level)
  local copies, waits for them, and re-layouts: 28.4 us -> 9.08 us
  waiting for transfers between devices: 83 us -> 102 us
  blocking collectives: 178 us -> 164 us
    reshape x4 -> x0, local copies, waits for them, and re-layouts: 14 us -> none  [the longest x2 7.08 us: rope_tables(): cos_full = jnp.stack([cos_t, cos_t], axis=-1).reshape(-1, HEAD_DIM)]
    select_n x0 -> x1, other arithmetic: none -> 13.7 us  [rope_tables(): return (jnp.cos(angles), jnp.where(lane % 2 == 0, -sin_t, sin_t))]
    psum x1 -> x0, blocking collectives: 13.6 us -> none  [layer(): d_lnw = lax.psum(d_lnw[0], 'sp').astype(jnp.bfloat16)]
    all_gather x1, waiting for transfers between devices: 61.9 us -> 74.9 us  [layer(): h_own = lax.all_gather(normed, 'sp', axis_index_groups=same_core)]
    pallas_call x1 -> x2, Pallas kernels: 30.8 us -> 35.3 us  [project(): pl.pallas_call(proj_kernel, grid_spec=pltpu.PrefetchScalarGridSpec(num_sc...]
    dot_general x2 -> x4, matrix products: 40.5 us -> 42.7 us  [wgrad(): jnp.einsum('ctd,cte->de', h, lax.dynamic_index_in_dim(blocks, c, 1, False...]
  transfers between devices with their start and end apart: 6 -> 8, of which waited for: 3 -> 3; matrix products, arithmetic and copies ran while one was open for 11% -> 9% of each run, Pallas kernels for 45% -> 47%
where the time goes in v4:
time: 733 us; the launch traced here: 723 us
  Pallas kernels  366 us (50%)
  blocking collectives  164 us (22%)
  waiting for transfers between devices  102 us (14%)
  matrix products  42.7 us (6%)
  other arithmetic  15.7 us (2%)
  between operations  14.2 us (2%)
  starting transfers between devices  9.57 us (1%)
  local copies, waits for them, and re-layouts  9.08 us (1%)
    all_to_all x2, blocking collectives, exchange(): return lax.all_to_all(x.reshape(sp_size, block, x.shape[1]), 'sp', 0, 0)  144 us
    pallas_call x2, Pallas kernels, attn_backward(): pl.pallas_call(bwd_kernel, grid=(rows // block,), in_specs=[q_spec, q_spe...  131 us
    pallas_call x1, Pallas kernels, attn_forward(): pl.pallas_call(fwd_kernel, grid=(heads, rows // block), in_specs=[pl.Bloc...  87.2 us
    all_gather x1, waiting for transfers between devices, layer(): h_own = lax.all_gather(normed, 'sp', axis_index_groups=same_core)  74.9 us
    pallas_call x2, Pallas kernels, tail(): pl.pallas_call(tail_b_kernel if last else tail_a_kernel, grid=(n,), in_sp...  46.2 us
    dot_general x4, matrix products, wgrad(): jnp.einsum('ctd,cte->de', h, lax.dynamic_index_in_dim(blocks, c, 1, False...  42.7 us
    pallas_call x2, Pallas kernels, project(): pl.pallas_call(proj_kernel, grid_spec=pltpu.PrefetchScalarGridSpec(num_sc...  35.3 us
    pallas_call x2, Pallas kernels, assemble(): pl.pallas_call(assemble_kernel, grid=(n,), in_specs=[pl.BlockSpec((1, row...  23.9 us
  transfers between devices with their start and end apart: 8, of which 3 were waited for; matrix products, arithmetic and copies ran while one was open for 9% of the time, Pallas kernels for 47%

profile of v4, /device:TPU:112, one launch (start us, length us, event | category | flops | bytes accessed | tf_op | source)
XLA Modules:
  0.0 723.3 jit_solution(11468804795877054055)
XLA Ops:
  7.2 0.1 all-gather.14.cloned.1.call-start
  7.2 1.3 broadcast_in_dim.33
  8.5 6.1 layer_norm.1
  14.6 0.0 copy-start.3
  14.6 0.1 all-gather.14.cloned.1.call-update
  14.7 0.1 all-gather.10.cloned.1.call-start
  14.8 0.7 all-gather.10.cloned.1.call-update
  15.5 0.1 all-gather.12.cloned.1.call-start
  15.6 0.0 copy-done.3
  15.6 20.2 %all-gather.3 = s32[8,1,768]{2,1,0:T(1,128)S(1)} all-gather(s32[1,1,768]{2,1,0:T(1,128)S(1)} %reshape.57), channel_id=1, replica_groups=mesh['dp'=2,'sp'=8] {'sp'}, dimensions={0}, use_global_device_ids=true | all-gather | bytes 27648 | tf_op jit(solution)/shard_map/all_gather | solution.py:428
  35.9 2.4 constant_dynamic-slice_fusion.w_ref
  38.3 2.3 constant_dynamic-slice_fusion.3.wq_ref
  40.5 3.1 constant_dynamic-slice_fusion.1
  43.6 13.7 %negate_select_fusion = (f32[6144,128]{1,0:T(8,128)}, f32[6144,128]{1,0:T(8,128)}) fusion(f32[128]{0:T(128)S(1)} %fusion.19, f32[6144]{0:T(1024)S(1)} %bitcast.50, pred[128]{0:T(512)(128)(4,1)S(1)} %broadcast_compare_fusion), kind=kLoop, calls=%fused_computation | loop fusion | flops 2359296 | bytes 6316672 | tf_op jit(solution)/shard_map/jit(_where)/select_n | solution.py:51
  57.3 74.9 %all-gather.14.cloned.1.call-done = bf16[3072,2048]{1,0:T(8,128)(2,1)} async-done(((bf16[768,2048]{1,0:T(8,128)(2,1)}), bf16[3072,2048]{1,0:T(8,128)(2,1)}) %all-gather.14.cloned.1.call-update) | async-done | bytes 12582928 | tf_op jit(solution)/shard_map/all_gather | solution.py:431
  132.2 0.0 collective-permute-start
  132.2 17.5 %project.2 = (bf16[6144,256]{1,0:T(8,128)(2,1)}, bf16[6144,256]{1,0:T(8,128)(2,1)}, bf16[6144,256]{1,0:T(8,128)(2,1)}, bf16[256,6144]{1,0:T(8,128)(2,1)}, bf16[256,6144]{1,0:T(8,128)(2,1)}) custom-call(s32[1]{0:T(128)} %bitcast.4.core_ref, bf16[4,768,2048]{2,1,0:T(8,128)(2,1)} %bitcast.55, bf16[2048,256]{1,0:T(8,128)(2,1)} %constant_dynamic-slice_fusion.3.wq_ref, ...), custom_call_target="tpu_custom_call" | custom-call | flops 9663676416 | bytes 20447232 | tf_op jit(solution)/shard_map/project/pallas_call | solution.py:92
  149.7 6.5 collective-permute-done.h_ref
  156.2 17.8 %project.3 = (bf16[6144,256]{1,0:T(8,128)(2,1)}, bf16[6144,256]{1,0:T(8,128)(2,1)}, bf16[6144,256]{1,0:T(8,128)(2,1)}, bf16[256,6144]{1,0:T(8,128)(2,1)}, bf16[256,6144]{1,0:T(8,128)(2,1)}) custom-call(s32[1]{0:T(128)} %bitcast.core_ref, ...), custom_call_target="tpu_custom_call", output_to_operand_aliasing={{0}: (7, {}), {1}: (8, {}), {2}: (9, {}), {3}: (10, {}), {4... | custom-call | flops 9663676416 | bytes 20447232 | tf_op jit(solution)/shard_map/project/pallas_call | solution.py:92
  174.1 87.2 %attn_fwd.1 = (bf16[6144,256]{1,0:T(8,128)(2,1)}, f32[256,6144]{1,0:T(8,128)}, f32[2,1,6144]{2,1,0:T(1,128)}) custom-call(bf16[6144,256]{1,0:T(8,128)(2,1)} %get-tuple-element.86.q_ref, bf16[6144,256]{1,0:T(8,128)(2,1)} %get-tuple-element.77.k_ref, bf16[256,6144]{1,0:T(8,128)(2,1)} %get-tuple-element.78.vt_ref), custom_call_target="tpu_custom_call" | custom-call | flops 38654705664 | bytes 15728640 | tf_op jit(solution)/shard_map/attn_fwd/pallas_call | solution.py:157
  261.3 0.0 all-gather.10.cloned.1.call-done.g_ref
  261.3 19.7 %cotangents.1 = (bf16[6144,256]{1,0:T(8,128)(2,1)}, bf16[256,2048]{1,0:T(8,128)(2,1)}) custom-call(bf16[6144,2048]{1,0:T(8,128)(2,1)} %all-gather.10.cloned.1.call-done.g_ref, bf16[256,2048]{1,0:T(8,128)(2,1)} %constant_dynamic-slice_fusion.w_ref, f32[256,6144]{1,0:T(8,128)} %get-tuple-element.79.ot_ref), custom_call_target="tpu_custom_call" | custom-call | flops 12884901888 | bytes 34603008 | tf_op jit(solution)/shard_map/cotangents/pallas_call | solution.py:284
  281.0 0.1 all-gather.12.cloned.1.call-update
  281.1 0.5 all-gather.16.cloned.1.call-start
  281.6 65.6 %attn_bwd.2 = bf16[6144,384]{1,0:T(8,128)(2,1)} custom-call(bf16[6144,256]{1,0:T(8,128)(2,1)} %get-tuple-element.86.q_ref, bf16[6144,256]{1,0:T(8,128)(2,1)} %get-tuple-element.82.do_ref, f32[256,6144]{1,0:T(8,128)} %get-tuple-element.79.ot_ref, f32[2,1,6144]{2,1,0:T(1,128)} %get-tuple-element.83.lse_ref, bf16[6144,256]{1,0:T(8,128)(2,1)} %get-tuple-element.77.k_ref, ...), custom_call_target="tpu_custom_call" | custom-call | flops 48318382080 | bytes 15728640 | tf_op jit(solution)/shard_map/attn_bwd/pallas_call | solution.py:245
  347.3 0.0 copy-start.1
  347.3 10.5 %fusion.6 = f32[2048,384,1]{1,0,2:T(8,128)S(1)} fusion(bf16[4,768,2048]{2,1,0:T(8,128)(2,1)} %bitcast.56, bf16[4,2,768,384]{3,2,1,0:T(8,128)(2,1)} %bitcast.46, s32[]{:T(128)S(6)} %select_n.44), kind=kOutput, calls=%fused_computation.11 | convolution fusion | flops 4831838208 | bytes 18087940 | tf_op jit(solution)/shard_map/ctd,cte->de/dot_general | solution.py:456
  357.8 0.0 copy-done.1
  357.8 10.8 %fusion.1 = bf16[2048,384]{1,0:T(8,128)(2,1)} fusion(f32[2048,384,1]{1,0,2:T(8,128)S(1)} %fusion.6, bf16[4,768,2048]{2,1,0:T(8,128)(2,1)} %collective-permute-done.h_ref, bf16[4,2,768,384]{3,2,1,0:T(8,128)(2,1)S(1)} %bitcast.48, s32[]{:T(128)S(6)} %select_n.45), kind=kOutput, calls=%fused_computation.6 | convolution fusion | flops 4833411072 | bytes 19660804 | tf_op jit(solution)/shard_map/ctd,cte->de/dot_general | solution.py:456
  368.6 0.1 all-gather.16.cloned.1.call-update
  368.7 0.2 all-gather.18.cloned.1.call-start
  368.9 65.7 %attn_bwd.3 = bf16[6144,384]{1,0:T(8,128)(2,1)} custom-call(bf16[6144,256]{1,0:T(8,128)(2,1)} %get-tuple-element.86.q_ref, bf16[6144,256]{1,0:T(8,128)(2,1)} %get-tuple-element.82.do_ref, f32[256,6144]{1,0:T(8,128)} %get-tuple-element.79.ot_ref, f32[2,1,6144]{2,1,0:T(1,128)} %get-tuple-element.83.lse_ref, bf16[6144,256]{1,0:T(8,128)(2,1)} %get-tuple-element.77.k_ref, ...), custom_call_target="tpu_custom_call" | custom-call | flops 48318382080 | bytes 15728640 | tf_op jit(solution)/shard_map/attn_bwd/pallas_call | solution.py:245
  434.6 0.0 copy-start
  434.6 10.5 %fusion.3 = f32[2048,384,1]{1,0,2:T(8,128)S(1)} fusion(bf16[4,768,2048]{2,1,0:T(8,128)(2,1)} %bitcast.57, bf16[4,2,768,384]{3,2,1,0:T(8,128)(2,1)} %bitcast.43, s32[]{:T(128)S(6)} %select_n.44), kind=kOutput, calls=%fused_computation.8 | convolution fusion | flops 4831838208 | bytes 18087940 | tf_op jit(solution)/shard_map/ctd,cte->de/dot_general | solution.py:456
  445.1 0.0 copy-done
  445.1 0.0 copy-start.2
  445.2 10.9 %fusion = bf16[2048,384]{1,0:T(8,128)(2,1)} fusion(f32[2048,384,1]{1,0,2:T(8,128)S(1)} %fusion.3, bf16[4,768,2048]{2,1,0:T(8,128)(2,1)} %collective-permute-done.h_ref, bf16[4,2,768,384]{3,2,1,0:T(8,128)(2,1)S(1)} %bitcast.45, s32[]{:T(128)S(6)} %select_n.45), kind=kOutput, calls=%fused_computation.4 | convolution fusion | flops 4833411072 | bytes 19660804 | tf_op jit(solution)/shard_map/ctd,cte->de/dot_general | solution.py:456
  456.0 0.1 all-gather.18.cloned.1.call-update
  456.1 0.0 copy-done.2
  456.1 73.4 %all_to_all.20.o_ref = bf16[8,768,256]{2,1,0:T(8,128)(2,1)} all-to-all(bf16[8,768,256]{2,1,0:T(8,128)(2,1)S(1)} %bitcast.49), channel_id=1, replica_groups=mesh['dp'=2,'sp'=8] {'sp'}, dimensions={0} | all-to-all | bytes 6291456 | tf_op jit(solution)/shard_map/all_to_all | solution.py:445
  529.5 70.4 %all_to_all.21.g_ref = bf16[8,768,384]{2,1,0:T(8,128)(2,1)} all-to-all(bf16[8,768,384]{2,1,0:T(8,128)(2,1)} %bitcast.47), channel_id=1, replica_groups=mesh['dp'=2,'sp'=8] {'sp'}, dimensions={0} | all-to-all | bytes 9437184 | tf_op jit(solution)/shard_map/all_to_all | solution.py:445
  599.9 5.1 all-to-all-start.2
  605.0 0.0 all-gather.12.cloned.1.call-done.slab_ref
  605.0 16.4 %out_project.1 = (bf16[768,2048]{1,0:T(8,128)(2,1)}, bf16[2048,2048]{1,0:T(8,128)(2,1)}) custom-call(bf16[8,768,256]{2,1,0:T(8,128)(2,1)} %all_to_all.20.o_ref, bf16[2048,2048]{1,0:T(8,128)(2,1)} %w_ref.1, bf16[2048,2048]{1,0:T(8,128)(2,1)} %all-gather.12.cloned.1.call-done.slab_ref), custom_call_target="tpu_custom_call" | custom-call | flops 6442450944 | bytes 11534336 | tf_op jit(solution)/shard_map/out_project/pallas_call | solution.py:314
  621.4 19.3 %tail_a.1.first_ref = f32[768,2048]{1,0:T(8,128)} custom-call(bf16[8,768,384]{2,1,0:T(8,128)(2,1)} %all_to_all.21.g_ref, bf16[2048,2048]{1,0:T(8,128)(2,1)} %wq_ref.3, bf16[2048,2048]{1,0:T(8,128)(2,1)} %wk_ref.3, bf16[2048,2048]{1,0:T(8,128)(2,1)} %wv_ref.3), custom_call_target="tpu_custom_call" | custom-call | flops 9663676416 | bytes 17301504 | tf_op jit(solution)/shard_map/tail_a/pallas_call | solution.py:383
  640.8 0.0 all-gather.16.cloned.1.call-done
  640.8 19.4 %all-to-all-done.2.g_ref = bf16[8,768,384]{2,1,0:T(8,128)(2,1)} async-done(((bf16[8,768,384]{2,1,0:T(8,128)(2,1)}), bf16[8,768,384]{2,1,0:T(8,128)(2,1)}, u32[]{:S(2)}, u32[]{:S(2)}) %all-to-all-start.2) | async-done | bytes 4718624 | tf_op jit(solution)/shard_map/all_to_all | solution.py:445
  660.2 26.9 %tail_b.1 = (bf16[768,2048]{1,0:T(8,128)(2,1)}, f32[1,2048]{1,0:T(1,128)}) custom-call(bf16[8,768,384]{2,1,0:T(8,128)(2,1)} %all-to-all-done.2.g_ref, bf16[2048,2048]{1,0:T(8,128)(2,1)} %wq_ref.3, bf16[2048,2048]{1,0:T(8,128)(2,1)} %wk_ref.3, bf16[2048,2048]{1,0:T(8,128)(2,1)} %wv_ref.3, f32[768,2048]{1,0:T(8,128)} %tail_a.1.first_ref, ...), custom_call_target="tpu_custom_call" | custom-call | flops 9663676416 | bytes 17301504 | tf_op jit(solution)/shard_map/tail_b/pallas_call | solution.py:383
  687.1 1.3 broadcast_in_dim.32
  688.4 3.6 all-to-all-start.3
  692.0 12.0 %assemble.2 = (bf16[2048,2048]{1,0:T(8,128)(2,1)}, bf16[2048,2048]{1,0:T(8,128)(2,1)}, bf16[2048,2048]{1,0:T(8,128)(2,1)}) custom-call(bf16[8,2048,384]{2,1,0:T(8,128)(2,1)} %bitcast.41), custom_call_target="tpu_custom_call" | custom-call | flops 402653184 | bytes 25165824 | tf_op jit(solution)/shard_map/assemble/pallas_call | solution.py:404
  704.0 0.0 all-gather.18.cloned.1.call-done
  704.0 12.0 %assemble.3 = (bf16[2048,2048]{1,0:T(8,128)(2,1)}, bf16[2048,2048]{1,0:T(8,128)(2,1)}, bf16[2048,2048]{1,0:T(8,128)(2,1)}) custom-call(bf16[8,2048,384]{2,1,0:T(8,128)(2,1)} %bitcast.42, bf16[2048,2048]{1,0:T(8,128)(2,1)} %get-tuple-element.110.refs_0_, ...), custom_call_target="tpu_custom_call", output_to_operand_aliasing={{0}: (1, {}), {1}: (2, {}), {2}: (3, {})} | custom-call | flops 402653184 | bytes 25165824 | tf_op jit(solution)/shard_map/assemble/pallas_call | solution.py:404
  715.9 0.0 all-to-all-done.3
  715.9 0.7 reduce_sum.9
  (4 shorter events, 0.0 us)
Async XLA Ops:
  7.2 125.0 %all-gather.14.cloned.1.call-start = ((), (), s32[]{:S(2)}) async-start(), calls=%async_computation.6 | async-start | bytes 15728640 | tf_op jit(solution)/shard_map/all_gather | solution.py:431
  14.6 1.0 copy-start.3
  14.7 246.6 %all-gather.10.cloned.1.call-start = ((), (), s32[]{:S(2)}) async-start(), calls=%async_computation.4 | async-start | bytes 28311552 | tf_op jit(solution)/shard_map/all_gather | solution.py:438
  15.5 589.5 %all-gather.12.cloned.1.call-start = ((), (), s32[]{:S(2)}) async-start(), calls=%async_computation.5 | async-start | bytes 9437184 | tf_op jit(solution)/shard_map/all_gather | solution.py:460
  132.2 24.0 %collective-permute-start = (bf16[4,768,2048]{2,1,0:T(8,128)(2,1)}, bf16[4,768,2048]{2,1,0:T(8,128)(2,1)}, u32[]{:S(2)}, u32[]{:S(2)}) collective-permute-start(bf16[4,768,2048]{2,1,0:T(8,128)(2,1)} %bitcast.54), channel_id=1, source_target_pairs={{0,1},{1,0},{2,3},{3,2},{4,5},{5,4},{6,7},{7,6},{8,9},{9,8},{10,11... | collective-permute-start | bytes 37748744 | tf_op jit(solution)/shard_map/ppermute | solution.py:437
  281.1 359.7 %all-gather.16.cloned.1.call-start = ((), (), s32[]{:S(2)}) async-start(), calls=%async_computation.7 | async-start | bytes 14155776 | tf_op jit(solution)/shard_map/all_gather | solution.py:465
  347.3 10.6 %copy-start.1 = (bf16[6144,384]{1,0:T(8,128)(2,1)S(1)}, bf16[6144,384]{1,0:T(8,128)(2,1)}, u32[]{:S(2)}) copy-start(bf16[6144,384]{1,0:T(8,128)(2,1)} %attn_bwd.2) | copy-start | bytes 14155780
  368.7 335.3 %all-gather.18.cloned.1.call-start = ((), (), s32[]{:S(2)}) async-start(), calls=%async_computation.8 | async-start | bytes 14155776 | tf_op jit(solution)/shard_map/all_gather | solution.py:470
  434.6 10.6 %copy-start = (bf16[6144,384]{1,0:T(8,128)(2,1)S(1)}, bf16[6144,384]{1,0:T(8,128)(2,1)}, u32[]{:S(2)}) copy-start(bf16[6144,384]{1,0:T(8,128)(2,1)} %attn_bwd.3) | copy-start | bytes 14155780
  445.1 10.9 %copy-start.2 = (bf16[6144,256]{1,0:T(8,128)(2,1)S(1)}, bf16[6144,256]{1,0:T(8,128)(2,1)}, u32[]{:S(2)}) copy-start(bf16[6144,256]{1,0:T(8,128)(2,1)} %get-tuple-element.87) | copy-start | bytes 9437188
  599.9 60.2 %all-to-all-start.2 = ((bf16[8,768,384]{2,1,0:T(8,128)(2,1)}), bf16[8,768,384]{2,1,0:T(8,128)(2,1)}, u32[]{:S(2)}, u32[]{:S(2)}) async-start(bf16[8,768,384]{2,1,0:T(8,128)(2,1)} %bitcast.44), calls=%async_computation.2 | async-start | bytes 9437184 | tf_op jit(solution)/shard_map/all_to_all | solution.py:445
  688.4 27.5 %all-to-all-start.3 = ((f32[8,1,2048]{2,1,0:T(1,128)}), f32[8,1,2048]{2,1,0:T(1,128)S(1)}, u32[]{:S(2)}, u32[]{:S(2)}) async-start(f32[8,1,2048]{2,1,0:T(1,128)} %broadcast_in_dim.32), calls=%async_computation.3 | async-start | bytes 131072 | tf_op jit(solution)/shard_map/all_to_all | solution.py:477
Sparse Core Ops, SparseCore 0:
  14.8 117.3 all-gather.13
  133.8 117.0 all-gather.9
  281.2 46.8 all-gather.11
  368.8 64.4 all-gather.15
  456.2 114.9 all-gather.17

commit v5 on v3

--- a/solution.py
+++ b/solution.py
@@ -44,12 +44,11 @@
 
 
 def rope_tables(positions):
-    inv_freq = ROPE_BASE ** (-jnp.arange(0, HEAD_DIM, 2, dtype=jnp.float32) / HEAD_DIM)
+    lane = jnp.arange(HEAD_DIM)
+    inv_freq = ROPE_BASE ** (-(lane - lane % 2).astype(jnp.float32) / HEAD_DIM)
     angles = positions.astype(jnp.float32)[:, None] * inv_freq[None, :]
-    cos_t, sin_t = jnp.cos(angles), jnp.sin(angles)
-    cos_full = jnp.stack([cos_t, cos_t], axis=-1).reshape(-1, HEAD_DIM)
-    sin_full = jnp.stack([-sin_t, sin_t], axis=-1).reshape(-1, HEAD_DIM)
-    return cos_full, sin_full
+    sin_t = jnp.sin(angles)
+    return jnp.cos(angles), jnp.where(lane % 2 == 0, -sin_t, sin_t)
 
 
 def swap_pairs(x):
@@ -176,12 +175,15 @@
 
 
 def bwd_kernel(q_ref, do_ref, ot_ref, lse_ref, k_ref, v_ref, kt_ref, cos_ref, sin_ref,
-               g_ref, dk_acc, dv_acc, dqt_acc):
+               g_ref, dk_acc, dv_acc, dqt_acc, cos_buf, sin_buf, sems):
     i = pl.program_id(0)
     rows = q_ref.shape[0]
+    fetches = [pltpu.make_async_copy(cos_ref, cos_buf, sems.at[0]), pltpu.make_async_copy(sin_ref, sin_buf, sems.at[1])]
 
     @pl.when(i == 0)
     def _():
+        for fetch in fetches:
+            fetch.start()
         dk_acc[...] = jnp.zeros_like(dk_acc)
         dv_acc[...] = jnp.zeros_like(dv_acc)
 
@@ -218,14 +220,20 @@
 
     lax.fori_loop(0, i, lambda j, c: (step(j, False), c)[1], 0)
     step(i, True)
+
+    @pl.when(i == 0)
+    def _():
+        for fetch in fetches:
+            fetch.wait()
+
     tile = pl.ds(pl.multiple_of(i * rows, rows), rows)
-    g_ref[tile, :HEAD_DIM] = unrope(dqt_acc[...].T, cos_ref[tile, :], sin_ref[tile, :])
+    g_ref[tile, :HEAD_DIM] = unrope(dqt_acc[...].T, cos_buf[tile, :], sin_buf[tile, :])
 
     @pl.when(i == pl.num_programs(0) - 1)
     def _():
         def finish(j, c):
             part = pl.ds(pl.multiple_of(j * rows, rows), rows)
-            g_ref[part, HEAD_DIM:2 * HEAD_DIM] = unrope(dk_acc[part, :], cos_ref[part, :], sin_ref[part, :])
+            g_ref[part, HEAD_DIM:2 * HEAD_DIM] = unrope(dk_acc[part, :], cos_buf[part, :], sin_buf[part, :])
             g_ref[part, 2 * HEAD_DIM:] = dv_acc[part, :].astype(jnp.bfloat16)
             return c
 
@@ -237,7 +245,7 @@
     flops = 2 * rows * rows * HEAD_DIM // 2
     q_spec = pl.BlockSpec((block, HEAD_DIM), lambda i: (i, head))
     all_spec = pl.BlockSpec((rows, HEAD_DIM), lambda i: (0, head))
-    table = pl.BlockSpec((rows, HEAD_DIM), lambda i: (0, 0))
+    table = pl.BlockSpec(memory_space=pl.ANY)
     return pl.pallas_call(
         bwd_kernel, grid=(rows // block,),
         in_specs=[q_spec, q_spec,
@@ -250,7 +258,10 @@
         out_shape=jax.ShapeDtypeStruct((rows, 3 * HEAD_DIM), jnp.bfloat16),
         scratch_shapes=[pltpu.VMEM((rows, HEAD_DIM), jnp.float32),
                         pltpu.VMEM((rows, HEAD_DIM), jnp.float32),
-                        pltpu.VMEM((HEAD_DIM, block), jnp.float32)],
+                        pltpu.VMEM((HEAD_DIM, block), jnp.float32),
+                        pltpu.VMEM((rows, HEAD_DIM), jnp.float32),
+                        pltpu.VMEM((rows, HEAD_DIM), jnp.float32),
+                        pltpu.SemaphoreType.DMA((2,))],
         compiler_params=pltpu.CompilerParams(vmem_limit_bytes=VMEM_LIMIT),
         cost_estimate=pl.CostEstimate(flops=2 * 5 * flops, bytes_accessed=20 * rows * HEAD_DIM, transcendentals=0),
         name="attn_bwd",
@@ -337,25 +348,30 @@
     add_head(g_ref, wq_ref, wk_ref, wv_ref, dh_ref)
 
 
-def tail_b_kernel(g_ref, wq_ref, wk_ref, wv_ref, first_ref, x_ref, lnw_ref, dx_ref, dlnw_ref, acc_ref):
+def tail_b_kernel(g_ref, wq_ref, wk_ref, wv_ref, first_ref, x_ref, lnw_ref, dx_ref, dlnw_ref, acc_ref, first_buf, x_buf, sems):
     d = pl.program_id(0)
+    fetches = [pltpu.make_async_copy(first_ref, first_buf, sems.at[0]), pltpu.make_async_copy(x_ref, x_buf, sems.at[1])]
 
     @pl.when(d == 0)
     def _():
-        acc_ref[...] = first_ref[...]
+        for fetch in fetches:
+            fetch.start()
+        acc_ref[...] = jnp.zeros_like(acc_ref)
 
     add_head(g_ref, wq_ref, wk_ref, wv_ref, acc_ref)
 
     @pl.when(d == pl.num_programs(0) - 1)
     def _():
+        for fetch in fetches:
+            fetch.wait()
         dlnw_ref[...] = jnp.zeros_like(dlnw_ref)
         lnw = lnw_ref[...]
         step = 64
 
         def rows_step(t, c):
             rows = pl.ds(pl.multiple_of(t * step, step), step)
-            x = x_ref[rows, :].astype(jnp.float32)
-            dh = acc_ref[rows, :]
+            x = x_buf[rows, :].astype(jnp.float32)
+            dh = acc_ref[rows, :] + first_buf[rows, :]
             centered = x - jnp.mean(x, axis=-1, keepdims=True)
             rstd = lax.rsqrt(jnp.mean(centered * centered, axis=-1, keepdims=True) + LN_EPS)
             xhat = centered * rstd
@@ -365,7 +381,7 @@
             dx_ref[rows, :] = dx.astype(jnp.bfloat16)
             return c
 
-        lax.fori_loop(0, x_ref.shape[0] // step, rows_step, 0)
+        lax.fori_loop(0, x_buf.shape[0] // step, rows_step, 0)
 
 
 def tail(g_chunks, w_q, w_k, w_v, head, heads, rest=()):
@@ -378,10 +394,11 @@
     last = bool(rest)
     return pl.pallas_call(
         tail_b_kernel if last else tail_a_kernel, grid=(n,),
-        in_specs=[pl.BlockSpec((1, rows, cols), lambda d: (d, 0, 0)), w_spec, w_spec, w_spec] + ([whole, whole, row] if last else []),
+        in_specs=[pl.BlockSpec((1, rows, cols), lambda d: (d, 0, 0)), w_spec, w_spec, w_spec] + ([pl.BlockSpec(memory_space=pl.ANY)] * 2 + [row] if last else []),
         out_specs=[whole, row] if last else whole,
         out_shape=[jax.ShapeDtypeStruct((rows, width), jnp.bfloat16), jax.ShapeDtypeStruct((1, width), jnp.float32)] if last else dh,
-        scratch_shapes=[pltpu.VMEM((rows, width), jnp.float32)] if last else [],
+        scratch_shapes=[pltpu.VMEM((rows, width), jnp.float32), pltpu.VMEM((rows, width), jnp.float32),
+                        pltpu.VMEM((rows, width), jnp.bfloat16), pltpu.SemaphoreType.DMA((2,))] if last else [],
         compiler_params=pltpu.CompilerParams(vmem_limit_bytes=VMEM_LIMIT),
         cost_estimate=pl.CostEstimate(flops=2 * n * rows * cols * width, bytes_accessed=2 * n * cols * (rows + width), transcendentals=0),
         name="tail_b" if last else "tail_a",
@@ -460,8 +477,9 @@
         dh_a, attn_out, dw_o, slab_a = lax.optimization_barrier((dh_a, attn_out, dw_o, slab_a))
         half = assemble(slab_a, 0, 2)
         d_hid, d_lnw = tail(gb_tok, w_q, w_k, w_v, 1, 2, (dh_a, hidden, lnw32[None]))
-        d_lnw = lax.psum(d_lnw[0], 'sp').astype(jnp.bfloat16)
-        half, d_hid, d_lnw, attn_out, slab_b = lax.optimization_barrier((half, d_hid, d_lnw, attn_out, slab_b))
+        parts = lax.all_to_all(jnp.broadcast_to(d_lnw[None], (sp_size,) + d_lnw.shape), 'sp', 0, 0)
+        d_lnw = jnp.sum(parts, axis=(0, 1)).astype(jnp.bfloat16)
+        half, d_hid, attn_out, slab_b = lax.optimization_barrier((half, d_hid, attn_out, slab_b))
         dw_q, dw_k, dw_v = assemble(slab_b, 1, 2, half)
         return attn_out, d_hid, d_lnw, dw_q, dw_k, dw_v, dw_o
 

time: 729 us -> 710 us (0.974); the launches traced: 720 us -> 709 us
  local copies, waits for them, and re-layouts: 28.4 us -> 9.05 us
  blocking collectives: 178 us -> 163 us
  waiting for transfers between devices: 83 us -> 97.4 us
    all_gather x1, waiting for transfers between devices: 61.9 us -> 76.6 us  [layer(): h_all = lax.all_gather(normed, 'sp', tiled=True)]
    reshape x4 -> x0, local copies, waits for them, and re-layouts: 14 us -> none  [the longest x2 7.08 us: rope_tables(): cos_full = jnp.stack([cos_t, cos_t], axis=-1).reshape(-1, HEAD_DIM)]
    select_n x0 -> x1, other arithmetic: none -> 13.7 us  [rope_tables(): return (jnp.cos(angles), jnp.where(lane % 2 == 0, -sin_t, sin_t))]
    psum x1 -> x0, blocking collectives: 13.6 us -> none  [layer(): d_lnw = lax.psum(d_lnw[0], 'sp').astype(jnp.bfloat16)]
  transfers between devices with their start and end apart: 6 -> 7, of which waited for: 3 -> 3; matrix products, arithmetic and copies ran while one was open for 11% -> 9% of each run, Pallas kernels for 45% -> 47%
where the time goes in v5:
time: 710 us; the launch traced here: 709 us
  Pallas kernels  359 us (51%)
  blocking collectives  163 us (23%)
  waiting for transfers between devices  97.4 us (14%)
  matrix products  40.5 us (6%)
  other arithmetic  15.7 us (2%)
  between operations  13.9 us (2%)
  starting transfers between devices  9.38 us (1%)
  local copies, waits for them, and re-layouts  9.05 us (1%)
    all_to_all x2, blocking collectives, exchange(): return lax.all_to_all(x.reshape(sp_size, block, x.shape[1]), 'sp', 0, 0)  143 us
    pallas_call x2, Pallas kernels, attn_backward(): pl.pallas_call(bwd_kernel, grid=(rows // block,), in_specs=[q_spec, q_spe...  132 us
    pallas_call x1, Pallas kernels, attn_forward(): pl.pallas_call(fwd_kernel, grid=(heads, rows // block), in_specs=[pl.Bloc...  87.1 us
    all_gather x1, waiting for transfers between devices, layer(): h_all = lax.all_gather(normed, 'sp', tiled=True)  76.6 us
    pallas_call x2, Pallas kernels, tail(): pl.pallas_call(tail_b_kernel if last else tail_a_kernel, grid=(n,), in_sp...  43.3 us
    dot_general x2, matrix products, wgrad(): jnp.einsum('td,te->de', h_all, x, preferred_element_type=jnp.float32)  40.5 us
    pallas_call x1, Pallas kernels, project(): pl.pallas_call(proj_kernel, grid=(rows // tile,), in_specs=[row_spec(dept...  30.8 us
    pallas_call x2, Pallas kernels, assemble(): pl.pallas_call(assemble_kernel, grid=(n,), in_specs=[pl.BlockSpec((1, row...  23.9 us
  transfers between devices with their start and end apart: 7, of which 3 were waited for; matrix products, arithmetic and copies ran while one was open for 9% of the time, Pallas kernels for 47%

profile of v5, /device:TPU:112, one launch (start us, length us, event | category | flops | bytes accessed | tf_op | source)
XLA Modules:
  0.0 708.5 jit_solution(6801049927062584780)
XLA Ops:
  7.2 0.1 all-gather.9.cloned.1.call-start
  7.2 1.3 broadcast_in_dim.25
  8.5 6.1 layer_norm.1
  14.6 0.0 copy-start.1
  14.6 0.1 all-gather.9.cloned.1.call-update
  14.7 0.1 all-gather.11.cloned.1.call-start
  14.8 0.7 all-gather.11.cloned.1.call-update
  15.5 0.1 all-gather.13.cloned.1.call-start
  15.6 0.0 copy-done.1
  15.6 20.2 %all-gather.2 = s32[8,1,768]{2,1,0:T(1,128)S(1)} all-gather(s32[1,1,768]{2,1,0:T(1,128)S(1)} %reshape.48), channel_id=1, replica_groups=mesh['dp'=2,'sp'=8] {'sp'}, dimensions={0}, use_global_device_ids=true | all-gather | bytes 27648 | tf_op jit(solution)/shard_map/all_gather | solution.py:441
  35.9 2.3 constant_dynamic-slice_fusion.w_ref
  38.2 2.3 constant_dynamic-slice_fusion.3.wq_ref
  40.5 3.1 constant_dynamic-slice_fusion.1
  43.6 13.7 %negate_select_fusion = (f32[6144,128]{1,0:T(8,128)}, f32[6144,128]{1,0:T(8,128)}) fusion(f32[128]{0:T(128)S(1)} %fusion.3, f32[6144]{0:T(1024)S(1)} %bitcast.17, pred[128]{0:T(512)(128)(4,1)S(1)} %broadcast_compare_fusion), kind=kLoop, calls=%fused_computation | loop fusion | flops 2359296 | bytes 6316672 | tf_op jit(solution)/shard_map/jit(_where)/select_n | solution.py:51
  57.3 76.6 %all-gather.9.cloned.1.call-done.h_ref = bf16[6144,2048]{1,0:T(8,128)(2,1)} async-done(((bf16[768,2048]{1,0:T(8,128)(2,1)}), bf16[6144,2048]{1,0:T(8,128)(2,1)}) %all-gather.9.cloned.1.call-update) | async-done | bytes 25165840 | tf_op jit(solution)/shard_map/all_gather | solution.py:442
  133.9 30.8 %project.1 = (bf16[6144,256]{1,0:T(8,128)(2,1)}, bf16[6144,256]{1,0:T(8,128)(2,1)}, bf16[6144,256]{1,0:T(8,128)(2,1)}, bf16[256,6144]{1,0:T(8,128)(2,1)}, bf16[256,6144]{1,0:T(8,128)(2,1)}) custom-call(bf16[6144,2048]{1,0:T(8,128)(2,1)} %all-gather.9.cloned.1.call-done.h_ref, bf16[2048,256]{1,0:T(8,128)(2,1)} %constant_dynamic-slice_fusion.3.wq_ref, ...), custom_call_target="tpu_custom_call" | custom-call | flops 19327352832 | bytes 40894464 | tf_op jit(solution)/shard_map/project/pallas_call | solution.py:91
  164.6 87.1 %attn_fwd.1 = (bf16[6144,256]{1,0:T(8,128)(2,1)}, f32[256,6144]{1,0:T(8,128)}, f32[2,1,6144]{2,1,0:T(1,128)}) custom-call(bf16[6144,256]{1,0:T(8,128)(2,1)} %get-tuple-element.58.q_ref, bf16[6144,256]{1,0:T(8,128)(2,1)} %get-tuple-element.49.k_ref, bf16[256,6144]{1,0:T(8,128)(2,1)} %get-tuple-element.50.vt_ref), custom_call_target="tpu_custom_call" | custom-call | flops 38654705664 | bytes 15728640 | tf_op jit(solution)/shard_map/attn_fwd/pallas_call | solution.py:152
  251.8 0.8 all-gather.11.cloned.1.call-done.g_ref
  252.5 19.7 %cotangents.1 = (bf16[6144,256]{1,0:T(8,128)(2,1)}, bf16[256,2048]{1,0:T(8,128)(2,1)}) custom-call(bf16[6144,2048]{1,0:T(8,128)(2,1)} %all-gather.11.cloned.1.call-done.g_ref, bf16[256,2048]{1,0:T(8,128)(2,1)} %constant_dynamic-slice_fusion.w_ref, f32[256,6144]{1,0:T(8,128)} %get-tuple-element.51.ot_ref), custom_call_target="tpu_custom_call" | custom-call | flops 12884901888 | bytes 34603008 | tf_op jit(solution)/shard_map/cotangents/pallas_call | solution.py:291
  272.2 0.1 all-gather.13.cloned.1.call-update
  272.3 0.2 all-gather.15.cloned.1.call-start
  272.6 65.9 %attn_bwd.2 = bf16[6144,384]{1,0:T(8,128)(2,1)} custom-call(bf16[6144,256]{1,0:T(8,128)(2,1)} %get-tuple-element.58.q_ref, bf16[6144,256]{1,0:T(8,128)(2,1)} %get-tuple-element.54.do_ref, f32[256,6144]{1,0:T(8,128)} %get-tuple-element.51.ot_ref, f32[2,1,6144]{2,1,0:T(1,128)} %get-tuple-element.55.lse_ref, bf16[6144,256]{1,0:T(8,128)(2,1)} %get-tuple-element.49.k_ref, ...), custom_call_target="tpu_custom_call" | custom-call | flops 48318382080 | bytes 15728640 | tf_op jit(solution)/shard_map/attn_bwd/pallas_call | solution.py:249
  338.5 20.2 %convolution_convert_fusion.1 = bf16[2048,384]{1,0:T(8,128)(2,1)} fusion(bf16[6144,2048]{1,0:T(8,128)(2,1)} %all-gather.9.cloned.1.call-done.h_ref, bf16[6144,384]{1,0:T(8,128)(2,1)} %attn_bwd.2), kind=kOutput, calls=%fused_computation.4 | convolution fusion | flops 9664462848 | bytes 31457280 | tf_op jit(solution)/shard_map/td,te->de/dot_general | solution.py:460
  358.7 0.1 all-gather.15.cloned.1.call-update
  358.7 0.3 all-gather.17.cloned.1.call-start
  359.0 66.0 %attn_bwd.3 = bf16[6144,384]{1,0:T(8,128)(2,1)} custom-call(bf16[6144,256]{1,0:T(8,128)(2,1)} %get-tuple-element.58.q_ref, bf16[6144,256]{1,0:T(8,128)(2,1)} %get-tuple-element.54.do_ref, f32[256,6144]{1,0:T(8,128)} %get-tuple-element.51.ot_ref, f32[2,1,6144]{2,1,0:T(1,128)} %get-tuple-element.55.lse_ref, bf16[6144,256]{1,0:T(8,128)(2,1)} %get-tuple-element.49.k_ref, ...), custom_call_target="tpu_custom_call" | custom-call | flops 48318382080 | bytes 15728640 | tf_op jit(solution)/shard_map/attn_bwd/pallas_call | solution.py:249
  425.0 0.0 copy-start
  425.0 20.3 %convolution_convert_fusion = bf16[2048,384]{1,0:T(8,128)(2,1)} fusion(bf16[6144,2048]{1,0:T(8,128)(2,1)} %all-gather.9.cloned.1.call-done.h_ref, bf16[6144,384]{1,0:T(8,128)(2,1)} %attn_bwd.3), kind=kOutput, calls=%fused_computation.3 | convolution fusion | flops 9664462848 | bytes 31457280 | tf_op jit(solution)/shard_map/td,te->de/dot_general | solution.py:460
  445.4 0.1 all-gather.17.cloned.1.call-update
  445.4 0.0 copy-done
  445.5 72.6 %all_to_all.20.o_ref = bf16[8,768,256]{2,1,0:T(8,128)(2,1)} all-to-all(bf16[8,768,256]{2,1,0:T(8,128)(2,1)S(1)} %bitcast.16), channel_id=1, replica_groups=mesh['dp'=2,'sp'=8] {'sp'}, dimensions={0} | all-to-all | bytes 6291456 | tf_op jit(solution)/shard_map/all_to_all | solution.py:450
  518.1 70.4 %all_to_all.21.g_ref = bf16[8,768,384]{2,1,0:T(8,128)(2,1)} all-to-all(bf16[8,768,384]{2,1,0:T(8,128)(2,1)} %bitcast.15), channel_id=1, replica_groups=mesh['dp'=2,'sp'=8] {'sp'}, dimensions={0} | all-to-all | bytes 9437184 | tf_op jit(solution)/shard_map/all_to_all | solution.py:450
  588.5 5.1 all-to-all-start.2
  593.6 0.0 all-gather.13.cloned.1.call-done.slab_ref
  593.6 16.4 %out_project.1 = (bf16[768,2048]{1,0:T(8,128)(2,1)}, bf16[2048,2048]{1,0:T(8,128)(2,1)}) custom-call(bf16[8,768,256]{2,1,0:T(8,128)(2,1)} %all_to_all.20.o_ref, bf16[2048,2048]{1,0:T(8,128)(2,1)} %w_ref.1, bf16[2048,2048]{1,0:T(8,128)(2,1)} %all-gather.13.cloned.1.call-done.slab_ref), custom_call_target="tpu_custom_call" | custom-call | flops 6442450944 | bytes 11534336 | tf_op jit(solution)/shard_map/out_project/pallas_call | solution.py:321
  610.0 19.3 %tail_a.1.first_ref = f32[768,2048]{1,0:T(8,128)} custom-call(bf16[8,768,384]{2,1,0:T(8,128)(2,1)} %all_to_all.21.g_ref, bf16[2048,2048]{1,0:T(8,128)(2,1)} %wq_ref.3, bf16[2048,2048]{1,0:T(8,128)(2,1)} %wk_ref.3, bf16[2048,2048]{1,0:T(8,128)(2,1)} %wv_ref.3), custom_call_target="tpu_custom_call" | custom-call | flops 9663676416 | bytes 17301504 | tf_op jit(solution)/shard_map/tail_a/pallas_call | solution.py:395
  629.4 0.0 all-gather.15.cloned.1.call-done
  629.4 19.1 %all-to-all-done.2.g_ref = bf16[8,768,384]{2,1,0:T(8,128)(2,1)} async-done(((bf16[8,768,384]{2,1,0:T(8,128)(2,1)}), bf16[8,768,384]{2,1,0:T(8,128)(2,1)}, u32[]{:S(2)}, u32[]{:S(2)}) %all-to-all-start.2) | async-done | bytes 4718624 | tf_op jit(solution)/shard_map/all_to_all | solution.py:450
  648.5 24.0 %tail_b.1 = (bf16[768,2048]{1,0:T(8,128)(2,1)}, f32[1,2048]{1,0:T(1,128)}) custom-call(bf16[8,768,384]{2,1,0:T(8,128)(2,1)} %all-to-all-done.2.g_ref, bf16[2048,2048]{1,0:T(8,128)(2,1)} %wq_ref.3, bf16[2048,2048]{1,0:T(8,128)(2,1)} %wk_ref.3, bf16[2048,2048]{1,0:T(8,128)(2,1)} %wv_ref.3, f32[768,2048]{1,0:T(8,128)} %tail_a.1.first_ref, ...), custom_call_target="tpu_custom_call" | custom-call | flops 9663676416 | bytes 17301504 | tf_op jit(solution)/shard_map/tail_b/pallas_call | solution.py:395
  672.5 1.3 broadcast_in_dim.24
  673.9 3.6 all-to-all-start.3
  677.4 12.0 %assemble.2 = (bf16[2048,2048]{1,0:T(8,128)(2,1)}, bf16[2048,2048]{1,0:T(8,128)(2,1)}, bf16[2048,2048]{1,0:T(8,128)(2,1)}) custom-call(bf16[8,2048,384]{2,1,0:T(8,128)(2,1)} %bitcast.12), custom_call_target="tpu_custom_call" | custom-call | flops 402653184 | bytes 25165824 | tf_op jit(solution)/shard_map/assemble/pallas_call | solution.py:417
  689.4 0.0 all-gather.17.cloned.1.call-done
  689.4 12.0 %assemble.3 = (bf16[2048,2048]{1,0:T(8,128)(2,1)}, bf16[2048,2048]{1,0:T(8,128)(2,1)}, bf16[2048,2048]{1,0:T(8,128)(2,1)}) custom-call(bf16[8,2048,384]{2,1,0:T(8,128)(2,1)} %bitcast.13, bf16[2048,2048]{1,0:T(8,128)(2,1)} %get-tuple-element.82.refs_0_, ...), custom_call_target="tpu_custom_call", output_to_operand_aliasing={{0}: (1, {}), {1}: (2, {}), {2}: (3, {})} | custom-call | flops 402653184 | bytes 25165824 | tf_op jit(solution)/shard_map/assemble/pallas_call | solution.py:417
  701.3 0.0 all-to-all-done.3
  701.4 0.7 reduce_sum.9
  (4 shorter events, 0.0 us)
Async XLA Ops:
  7.2 126.7 %all-gather.9.cloned.1.call-start = ((), (), s32[]{:S(2)}) async-start(), calls=%async_computation.4 | async-start | bytes 28311552 | tf_op jit(solution)/shard_map/all_gather | solution.py:442
  14.6 1.0 copy-start.1
  14.7 237.8 %all-gather.11.cloned.1.call-start = ((), (), s32[]{:S(2)}) async-start(), calls=%async_computation.5 | async-start | bytes 28311552 | tf_op jit(solution)/shard_map/all_gather | solution.py:443
  15.5 578.1 %all-gather.13.cloned.1.call-start = ((), (), s32[]{:S(2)}) async-start(), calls=%async_computation.6 | async-start | bytes 9437184 | tf_op jit(solution)/shard_map/all_gather | solution.py:463
  272.3 357.1 %all-gather.15.cloned.1.call-start = ((), (), s32[]{:S(2)}) async-start(), calls=%async_computation.7 | async-start | bytes 14155776 | tf_op jit(solution)/shard_map/all_gather | solution.py:468
  358.7 330.7 %all-gather.17.cloned.1.call-start = ((), (), s32[]{:S(2)}) async-start(), calls=%async_computation.8 | async-start | bytes 14155776 | tf_op jit(solution)/shard_map/all_gather | solution.py:473
  425.0 20.4 %copy-start = (bf16[6144,256]{1,0:T(8,128)(2,1)S(1)}, bf16[6144,256]{1,0:T(8,128)(2,1)}, u32[]{:S(2)}) copy-start(bf16[6144,256]{1,0:T(8,128)(2,1)} %get-tuple-element.59) | copy-start | bytes 9437188
  588.5 60.0 %all-to-all-start.2 = ((bf16[8,768,384]{2,1,0:T(8,128)(2,1)}), bf16[8,768,384]{2,1,0:T(8,128)(2,1)}, u32[]{:S(2)}, u32[]{:S(2)}) async-start(bf16[8,768,384]{2,1,0:T(8,128)(2,1)} %bitcast.14), calls=%async_computation.2 | async-start | bytes 9437184 | tf_op jit(solution)/shard_map/all_to_all | solution.py:450
  673.9 27.5 %all-to-all-start.3 = ((f32[8,1,2048]{2,1,0:T(1,128)}), f32[8,1,2048]{2,1,0:T(1,128)S(1)}, u32[]{:S(2)}, u32[]{:S(2)}) async-start(f32[8,1,2048]{2,1,0:T(1,128)} %broadcast_in_dim.24), calls=%async_computation.3 | async-start | bytes 131072 | tf_op jit(solution)/shard_map/all_to_all | solution.py:480
Sparse Core Ops, SparseCore 0:
  14.8 119.0 all-gather.8
  135.4 117.0 all-gather.10
  272.4 46.5 all-gather.12
  358.8 63.9 all-gather.14
  445.6 114.0 all-gather.16
